TPU v7x, 16 devices: a whole 2x2x2 slice. The times are simulated.
16 devices in a mesh: model: 4 (over z, y), data: 4 (over x, core).
Axes of the slice: x: 2, y: 2, z: 2, core: 2. Of those that a mesh axis runs over, the one named last changes fastest.
Arguments:
- grad_qkv: float32 [4, 32, 256, 768], P('data', None, None, 'model')
- weight_qkv: float32 [32, 256, 768], P(None, 'data', 'model')
- moment1_qkv: float32 [32, 256, 768], P(None, 'data', 'model')
- moment2_qkv: float32 [32, 256, 768], P(None, 'data', 'model')
- grad_proj: float32 [4, 32, 256, 256], P('data', None, 'model')
- weight_proj: float32 [32, 256, 256], P(None, ('model', 'data'))
- moment1_proj: float32 [32, 256, 256], P(None, ('model', 'data'))
- moment2_proj: float32 [32, 256, 256], P(None, ('model', 'data'))
- grad_fcin: float32 [4, 32, 256, 1024], P('data', None, None, 'model')
- weight_fcin: float32 [32, 256, 1024], P(None, 'data', 'model')
- moment1_fcin: float32 [32, 256, 1024], P(None, 'data', 'model')
- moment2_fcin: float32 [32, 256, 1024], P(None, 'data', 'model')
- grad_fcout: float32 [4, 32, 1024, 256], P('data', None, 'model')
- weight_fcout: float32 [32, 1024, 256], P(None, ('model', 'data'))
- moment1_fcout: float32 [32, 1024, 256], P(None, ('model', 'data'))
- moment2_fcout: float32 [32, 1024, 256], P(None, ('model', 'data'))
Outputs:
- output 1: bfloat16 [32, 256, 768], P(None, None, 'model')
- output 2: bfloat16 [32, 256, 256], P(None, 'model')
- output 3: bfloat16 [32, 256, 1024], P(None, None, 'model')
- output 4: bfloat16 [32, 1024, 256], P(None, 'model')
- output 5: float32 [32, 256, 768], P(None, 'data', 'model')
- output 6: float32 [32, 256, 256], P(None, ('model', 'data'))
- output 7: float32 [32, 256, 1024], P(None, 'data', 'model')
- output 8: float32 [32, 1024, 256], P(None, ('model', 'data'))
- output 9: float32 [32, 256, 768], P(None, 'data', 'model')
- output 10: float32 [32, 256, 256], P(None, ('model', 'data'))
- output 11: float32 [32, 256, 1024], P(None, 'data', 'model')
- output 12: float32 [32, 1024, 256], P(None, ('model', 'data'))
- output 13: float32 [32, 256, 768], P(None, 'data', 'model')
- output 14: float32 [32, 256, 256], P(None, ('model', 'data'))
- output 15: float32 [32, 256, 1024], P(None, 'data', 'model')
- output 16: float32 [32, 1024, 256], P(None, ('model', 'data'))
All inputs are finite; a program needn't handle non-finite values.
Results may differ from a plain program's by a relative error of at most 0.001.
Values are sent between devices in bfloat16 or wider.
A program may use at most 1 GiB of HBM per device.

v0:
```python
import jax
import jax.numpy as jnp
from jax import lax
from jax.sharding import PartitionSpec as P

LEARN_RATE = 0.08
BETA_ONE = 0.9
BETA_TWO = 0.999
ADAM_EPS = 1e-6
DECAY_RATE = 0.01
MAX_NORM = 1.0
STEP_COUNT = 100
COLUMN_SPLIT = (True, False, True, False)


def grad_spec(col_split):
    return P("data", None, None, "model") if col_split else P("data", None, "model", None)


def state_spec(col_split):
    return P(None, "data", "model") if col_split else P(None, ("model", "data"), None)


def replica_spec(col_split):
    return P(None, None, "model") if col_split else P(None, "model", None)


def adam_direction(grad_mean, weight, moment1, moment2, clip_coef):
    clipped = clip_coef * grad_mean
    new_first = BETA_ONE * moment1 + (1.0 - BETA_ONE) * clipped
    new_second = BETA_TWO * moment2 + (1.0 - BETA_TWO) * clipped * clipped
    first_hat = new_first / (1.0 - BETA_ONE ** STEP_COUNT)
    second_hat = new_second / (1.0 - BETA_TWO ** STEP_COUNT)
    update = first_hat / (jnp.sqrt(second_hat) + ADAM_EPS) + DECAY_RATE * weight
    return update, new_first, new_second


def solution(mesh):
    group_size = mesh.shape["data"]
    in_specs = []
    for col_split in COLUMN_SPLIT:
        in_specs.extend([grad_spec(col_split), state_spec(col_split), state_spec(col_split), state_spec(col_split)])
    out_specs = tuple([replica_spec(col_split) for col_split in COLUMN_SPLIT] + [state_spec(col_split) for col_split in COLUMN_SPLIT] * 3)

    def device_step(*arrays):
        kind_count = len(COLUMN_SPLIT)
        grad_means = []
        for kind_idx in range(kind_count):
            sent_grad = arrays[4 * kind_idx].astype(jnp.bfloat16)
            received = lax.all_to_all(sent_grad, "data", 2, 0, tiled=True)
            grad_means.append(jnp.sum(received, axis=0, dtype=jnp.float32) / group_size)
        local_sq = sum(jnp.sum(grad_mean * grad_mean) for grad_mean in grad_means)
        total_norm = jnp.sqrt(lax.psum(local_sq, ("model", "data")))
        clip_coef = jnp.minimum(1.0, MAX_NORM / total_norm)
        replicas, weights, firsts, seconds = [], [], [], []
        for kind_idx in range(kind_count):
            weight = arrays[4 * kind_idx + 1]
            update, new_first, new_second = adam_direction(grad_means[kind_idx], weight, arrays[4 * kind_idx + 2], arrays[4 * kind_idx + 3], clip_coef)
            sq_pair = jnp.stack([jnp.sum(weight * weight, axis=(1, 2)), jnp.sum(update * update, axis=(1, 2))])
            norm_pair = jnp.sqrt(lax.psum(sq_pair, ("model", "data")))
            trust_ratio = (norm_pair[0] / norm_pair[1])[:, None, None]
            new_weight = weight - LEARN_RATE * trust_ratio * update
            replicas.append(lax.all_gather(new_weight.astype(jnp.bfloat16), "data", axis=1, tiled=True))
            weights.append(new_weight)
            firsts.append(new_first)
            seconds.append(new_second)
        return tuple(replicas + weights + firsts + seconds)

    return jax.shard_map(device_step, mesh=mesh, in_specs=tuple(in_specs), out_specs=out_specs, check_vma=False)
```

profile of v0, /device:TPU:0, one launch (start us, length us, event | category | flops | bytes accessed | tf_op | source)
XLA Modules:
  0.0 420.7 jit_solution(3324957486786724162)
XLA Ops:
  7.2 3.7 copy.160
  10.9 4.5 %all-to-all-start.1 = ((bf16[1,32,64,256]{3,1,0,2:T(8,128)(2,1)}), bf16[1,32,64,256]{3,1,0,2:T(8,128)(2,1)}, u32[]{:S(2)}, u32[]{:S(2)}) async-start(bf16[1,32,64,256]{3,1,0,2:T(8,128)(2,1)} %copy.160), calls=%async_computation.1 | async-start | bytes 2097152 | tf_op jit(solution)/shard_map/all_to_all | solution.py:50
  15.4 3.2 convert_element_type.56
  18.6 5.5 %copy.101 = bf16[1,32,256,192]{3,1,0,2:T(8,128)(2,1)} copy(bf16[1,32,256,192]{2,3,1,0:T(8,128)(2,1)S(1)} %convert_element_type.56) | data formatting | bytes 6291456 | tf_op jit(solution)/shard_map/convert_element_type | solution.py:49
  24.1 6.1 %all-to-all-done.1 = bf16[1,32,64,256]{3,1,0,2:T(8,128)(2,1)} async-done(((bf16[1,32,64,256]{3,1,0,2:T(8,128)(2,1)}), bf16[1,32,64,256]{3,1,0,2:T(8,128)(2,1)}, u32[]{:S(2)}, u32[]{:S(2)}) %all-to-all-start.1) | async-done | bytes 1048608 | tf_op jit(solution)/shard_map/all_to_all | solution.py:50
  30.2 4.9 %all-to-all-start = ((bf16[1,32,256,192]{3,1,0,2:T(8,128)(2,1)}), bf16[1,32,256,192]{3,1,0,2:T(8,128)(2,1)}, u32[]{:S(2)}, u32[]{:S(2)}) async-start(bf16[1,32,256,192]{3,1,0,2:T(8,128)(2,1)} %copy.101), calls=%async_computation | async-start | bytes 8388608 | tf_op jit(solution)/shard_map/all_to_all | solution.py:50
  35.1 9.8 %copy.159 = bf16[1,32,256,256]{3,1,0,2:T(8,128)(2,1)} copy(f32[1,32,256,256]{3,2,1,0:T(8,128)} %param.24) | data formatting | bytes 12582912 | tf_op args[8]
  44.9 38.0 %all-to-all-done = bf16[1,32,256,192]{3,1,0,2:T(8,128)(2,1)} async-done(((bf16[1,32,256,192]{3,1,0,2:T(8,128)(2,1)}), bf16[1,32,256,192]{3,1,0,2:T(8,128)(2,1)}, u32[]{:S(2)}, u32[]{:S(2)}) %all-to-all-start) | async-done | bytes 3145760 | tf_op jit(solution)/shard_map/all_to_all | solution.py:50
  83.0 5.1 %all-to-all-start.2 = ((bf16[1,32,256,256]{3,1,0,2:T(8,128)(2,1)}), bf16[1,32,256,256]{3,1,0,2:T(8,128)(2,1)}, u32[]{:S(2)}, u32[]{:S(2)}) async-start(bf16[1,32,256,256]{3,1,0,2:T(8,128)(2,1)} %copy.159), calls=%async_computation.2 | async-start | bytes 8388608 | tf_op jit(solution)/shard_map/all_to_all | solution.py:50
  88.1 9.8 %copy.158 = bf16[1,32,256,256]{3,1,0,2:T(8,128)(2,1)} copy(f32[1,32,256,256]{3,2,1,0:T(8,128)} %param.28) | data formatting | bytes 12582912 | tf_op args[12]
  98.0 38.0 %all-to-all-done.2 = bf16[1,32,256,256]{3,1,0,2:T(8,128)(2,1)} async-done(((bf16[1,32,256,256]{3,1,0,2:T(8,128)(2,1)}), bf16[1,32,256,256]{3,1,0,2:T(8,128)(2,1)}, u32[]{:S(2)}, u32[]{:S(2)}) %all-to-all-start.2) | async-done | bytes 4194336 | tf_op jit(solution)/shard_map/all_to_all | solution.py:50
  136.0 4.9 %all-to-all-start.3 = ((bf16[1,32,256,256]{3,1,0,2:T(8,128)(2,1)}), bf16[1,32,256,256]{3,1,0,2:T(8,128)(2,1)}, u32[]{:S(2)}, u32[]{:S(2)}) async-start(bf16[1,32,256,256]{3,1,0,2:T(8,128)(2,1)} %copy.158), calls=%async_computation.3 | async-start | bytes 8388608 | tf_op jit(solution)/shard_map/all_to_all | solution.py:50
  140.9 0.0 copy-start.3
  140.9 0.6 all-gather.7.cloned.1.call-start
  141.5 2.0 multiply_reduce_fusion.3
  143.5 0.3 multiply_reduce_fusion.1
  143.8 1.5 convert_reduce_fusion.3
  145.3 0.7 multiply_reduce_fusion.11
  146.0 4.6 %copy.102 = bf16[1,32,256,192]{3,2,1,0:T(8,128)(2,1)S(1)} copy(bf16[1,32,256,192]{3,1,0,2:T(8,128)(2,1)} %all-to-all-done) | data formatting | bytes 6291456 | tf_op jit(solution)/shard_map/all_to_all | solution.py:50
  150.6 0.9 convert_reduce_fusion.2
  151.5 1.1 multiply_reduce_fusion.7
  153.9 3.4 convert_reduce_fusion.1
  157.3 0.0 copy-start
  157.3 1.3 copy-done
  158.6 1.1 multiply_reduce_fusion.6
  159.8 29.0 %all-to-all-done.3 = bf16[1,32,256,256]{3,1,0,2:T(8,128)(2,1)} async-done(((bf16[1,32,256,256]{3,1,0,2:T(8,128)(2,1)}), bf16[1,32,256,256]{3,1,0,2:T(8,128)(2,1)}, u32[]{:S(2)}, u32[]{:S(2)}) %all-to-all-start.3) | async-done | bytes 4194336 | tf_op jit(solution)/shard_map/all_to_all | solution.py:50
  188.8 3.4 convert_reduce_fusion
  192.2 0.0 copy-start.2
  192.2 1.3 copy-done.2
  193.6 1.1 multiply_reduce_fusion.5
  196.0 0.3 multiply_reduce_fusion.10
  196.3 32.9 %psum.35 = f32[]{:T(128)} all-reduce(f32[]{:T(128)S(6)} %add.75), channel_id=1, replica_groups=mesh['model'=4,'data'=4] {'model','data'}, use_global_device_ids=true, to_apply=%region_9.0 | all-reduce | flops 1 | bytes 8 | tf_op jit(solution)/shard_map/psum | solution.py:53
  229.9 0.0 copy-start.1
  229.9 3.6 multiply_reduce_fusion.9
  233.5 16.8 %multiply_reduce_fusion = (f32[32]{0:T(128)S(1)}, f32[32,64,256]{2,0,1:T(8,128)}, f32[32,64,256]{2,0,1:T(8,128)}, f32[32,64,256]{2,0,1:T(8,128)}, f32[32]{0:T(12...) fusion(f32[32,64,256]{2,1,0:T(8,128)} %param.29, f32[32,64,256]{2,0,1:T(8,128)} %copy-done.2, ...), kind=kLoop, calls=%fused_computation.20 | loop fusion | flops 16777152 | bytes 29360388 | tf_op jit(solution)/shard_map/reduce_sum | solution.py:59
  250.4 3.9 multiply_reduce_fusion.8
  254.3 32.7 %all-reduce = (f32[2,32]{1,0:T(2,128)S(1)}, f32[2,32]{1,0:T(2,128)S(1)}, f32[2,32]{1,0:T(2,128)S(1)}, f32[2,32]{1,0:T(2,128)S(1)}) all-reduce(f32[2,32]{1,0:T(2,128)S(1)} %get-tuple-element.144, f32[2,32]{1,0:T(2,128)S(1)} %get-tuple-element.145, ...), channel_id=1, replica_groups=mesh['model'=4,'data'=4] {'model','data'}, use_global_device_ids=true, to_apply=%region_11.0 | all-reduce | flops 256 | bytes 2048 | tf_op jit(solution)/shard_map/psum | solution.py:60
  287.0 2.1 fusion.9
  289.1 0.0 all-gather.7.cloned.1.call-update
  289.1 0.3 all-gather.5.cloned.1.call-start
  289.4 5.9 %fusion.10 = (bf16[32,64,192]{2,1,0:T(8,128)(2,1)}, f32[32,64,192]{2,1,0:T(8,128)}) fusion(f32[32,64,192]{2,1,0:T(8,128)} %param.17, f32[32,64,192]{2,1,0:T(8,128)} %get-tuple-element.139, f32[32,64,192]{2,1,0:T(8,128)} %get-tuple-element.138, f32[32]{0:T(128)S(1)} %multiply_bitcast_fusion.3), kind=kLoop, calls=%fused_computation.60 | loop fusion | flops 3538944 | bytes 7078016 | tf_op jit(solution)/shard_map/convert_element_type | solution.py:63
  295.3 0.0 all-gather.5.cloned.1.call-update
  295.3 0.0 all-gather.11.cloned.1.call-start
  295.4 4.6 %fusion.7 = (bf16[32,64,256]{2,0,1:T(8,128)(2,1)}, f32[32,64,256]{2,0,1:T(8,128)}) fusion(f32[32,64,256]{2,0,1:T(8,128)} %get-tuple-element.127, f32[32]{0:T(128)S(1)} %multiply_bitcast_fusion, f32[32,64,256]{2,1,0:T(8,128)S(1)} %copy-done.4), kind=kLoop, calls=%fused_computation.57 | loop fusion | flops 1572864 | bytes 7340160 | tf_op jit(solution)/shard_map/convert_element_type | solution.py:63
  300.0 0.0 all-gather.11.cloned.1.call-update
  300.0 0.0 all-gather.9.cloned.1.call-start
  300.1 5.3 %fusion.8 = (bf16[32,64,256]{2,0,1:T(8,128)(2,1)}, f32[32,64,256]{2,0,1:T(8,128)}) fusion(f32[32,64,256]{2,0,1:T(8,128)} %get-tuple-element.141, f32[32]{0:T(128)S(1)} %multiply_bitcast_fusion.1, f32[32,64,256]{2,1,0:T(8,128)} %param.25), kind=kLoop, calls=%fused_computation.58 | loop fusion | flops 1572864 | bytes 7340160 | tf_op jit(solution)/shard_map/convert_element_type | solution.py:63
  305.4 0.0 all-gather.9.cloned.1.call-update
  305.5 2.5 copy.124
  308.0 2.5 copy.123
  310.6 1.1 copy.122
  311.7 2.5 copy.126
  314.2 2.5 copy.127
  316.8 2.5 copy.129
  319.3 2.5 copy.130
  321.8 1.1 copy.125
  322.9 1.1 copy.128
  324.1 2.8 copy.119
  326.8 12.5 %all-gather.5.cloned.1.call-done = bf16[32,256,192]{2,1,0:T(8,128)(2,1)} async-done(((bf16[32,64,192]{2,1,0:T(8,128)(2,1)}), bf16[32,256,192]{2,1,0:T(8,128)(2,1)}) %all-gather.5.cloned.1.call-update) | async-done | bytes 3145744 | tf_op jit(solution)/shard_map/all_gather | solution.py:63
  339.4 6.4 %copy.118 = bf16[32,256,192]{1,2,0:T(8,128)(2,1)} copy(bf16[32,256,192]{2,1,0:T(8,128)(2,1)} %all-gather.5.cloned.1.call-done) | data formatting | bytes 6291456
  345.7 27.6 %all-gather.11.cloned.1.call-done = bf16[32,256,256]{2,0,1:T(8,128)(2,1)} async-done(((bf16[32,64,256]{2,0,1:T(8,128)(2,1)}), bf16[32,256,256]{2,0,1:T(8,128)(2,1)}) %all-gather.11.cloned.1.call-update) | async-done | bytes 4194320 | tf_op jit(solution)/shard_map/all_gather | solution.py:63
  373.3 6.6 %copy.121 = bf16[32,256,256]{2,1,0:T(8,128)(2,1)} copy(bf16[32,256,256]{2,0,1:T(8,128)(2,1)} %all-gather.11.cloned.1.call-done) | data formatting | bytes 8388608
  379.9 27.3 %all-gather.9.cloned.1.call-done = bf16[32,256,256]{2,0,1:T(8,128)(2,1)} async-done(((bf16[32,64,256]{2,0,1:T(8,128)(2,1)}), bf16[32,256,256]{2,0,1:T(8,128)(2,1)}) %all-gather.9.cloned.1.call-update) | async-done | bytes 4194320 | tf_op jit(solution)/shard_map/all_gather | solution.py:63
  407.2 6.6 %copy.120 = bf16[32,256,256]{2,1,0:T(8,128)(2,1)} copy(bf16[32,256,256]{2,0,1:T(8,128)(2,1)} %all-gather.9.cloned.1.call-done) | data formatting | bytes 8388608
  (40 shorter events, 0.2 us)
Async XLA Ops:
  10.9 19.4 %all-to-all-start.1 = ((bf16[1,32,64,256]{3,1,0,2:T(8,128)(2,1)}), bf16[1,32,64,256]{3,1,0,2:T(8,128)(2,1)}, u32[]{:S(2)}, u32[]{:S(2)}) async-start(bf16[1,32,64,256]{3,1,0,2:T(8,128)(2,1)} %copy.160), calls=%async_computation.1 | async-start | bytes 2097152 | tf_op jit(solution)/shard_map/all_to_all | solution.py:50
  30.2 52.8 %all-to-all-start = ((bf16[1,32,256,192]{3,1,0,2:T(8,128)(2,1)}), bf16[1,32,256,192]{3,1,0,2:T(8,128)(2,1)}, u32[]{:S(2)}, u32[]{:S(2)}) async-start(bf16[1,32,256,192]{3,1,0,2:T(8,128)(2,1)} %copy.101), calls=%async_computation | async-start | bytes 8388608 | tf_op jit(solution)/shard_map/all_to_all | solution.py:50
  83.0 53.0 %all-to-all-start.2 = ((bf16[1,32,256,256]{3,1,0,2:T(8,128)(2,1)}), bf16[1,32,256,256]{3,1,0,2:T(8,128)(2,1)}, u32[]{:S(2)}, u32[]{:S(2)}) async-start(bf16[1,32,256,256]{3,1,0,2:T(8,128)(2,1)} %copy.159), calls=%async_computation.2 | async-start | bytes 8388608 | tf_op jit(solution)/shard_map/all_to_all | solution.py:50
  136.0 52.8 %all-to-all-start.3 = ((bf16[1,32,256,256]{3,1,0,2:T(8,128)(2,1)}), bf16[1,32,256,256]{3,1,0,2:T(8,128)(2,1)}, u32[]{:S(2)}, u32[]{:S(2)}) async-start(bf16[1,32,256,256]{3,1,0,2:T(8,128)(2,1)} %copy.158), calls=%async_computation.3 | async-start | bytes 8388608 | tf_op jit(solution)/shard_map/all_to_all | solution.py:50
  140.9 2.6 copy-start.3
  140.9 183.1 %all-gather.7.cloned.1.call-start = ((), (), s32[]{:S(2)}) async-start(), calls=%async_computation.5 | async-start | bytes 1310720 | tf_op jit(solution)/shard_map/all_gather | solution.py:63
  157.3 1.3 copy-start
  192.2 1.3 copy-start.2
  193.5 2.4 copy-start.12
  229.9 3.6 copy-start.1
  233.5 16.9 %copy-start.5 = (f32[32,64,192]{2,1,0:T(8,128)S(1)}, f32[32,64,192]{2,1,0:T(8,128)}, u32[]{:S(2)}) copy-start(f32[32,64,192]{2,1,0:T(8,128)} %param.17) | copy-start | bytes 4718596
  233.5 16.9 %copy-start.13 = (f32[32,64,192]{2,1,0:T(8,128)S(1)}, f32[32,64,192]{2,1,0:T(8,128)}, u32[]{:S(2)}) copy-start(f32[32,64,192]{2,1,0:T(8,128)} %param.18) | copy-start | bytes 4718596
  233.5 16.8 %copy-start.14 = (f32[32,64,192]{2,1,0:T(8,128)S(1)}, f32[32,64,192]{2,1,0:T(8,128)}, u32[]{:S(2)}) copy-start(f32[32,64,192]{2,1,0:T(8,128)} %param.19) | copy-start | bytes 4718596
  289.1 50.2 %all-gather.5.cloned.1.call-start = ((), (), s32[]{:S(2)}) async-start(), calls=%async_computation.4 | async-start | bytes 5242880 | tf_op jit(solution)/shard_map/all_gather | solution.py:63
  289.4 6.0 %copy-start.4 = (f32[32,64,256]{2,1,0:T(8,128)S(1)}, f32[32,64,256]{2,1,0:T(8,128)}, u32[]{:S(2)}) copy-start(f32[32,64,256]{2,1,0:T(8,128)} %param.29) | copy-start | bytes 6291460
  295.3 78.0 %all-gather.11.cloned.1.call-start = ((), (), s32[]{:S(2)}) async-start(), calls=%async_computation.7 | async-start | bytes 5242880 | tf_op jit(solution)/shard_map/all_gather | solution.py:63
  300.0 107.2 %all-gather.9.cloned.1.call-start = ((), (), s32[]{:S(2)}) async-start(), calls=%async_computation.6 | async-start | bytes 5242880 | tf_op jit(solution)/shard_map/all_gather | solution.py:63
  300.1 5.4 %copy-start.10 = (f32[32,64,256]{2,0,1:T(8,128)S(1)}, f32[32,64,256]{2,0,1:T(8,128)}, u32[]{:S(2)}) copy-start(f32[32,64,256]{2,0,1:T(8,128)} %get-tuple-element.119) | copy-start | bytes 6291460
  305.5 2.6 copy-start.11
  308.0 3.6 copy-start.9
  311.7 2.5 copy-start.8
  314.2 2.5 copy-start.7
  316.8 2.5 copy-start.6
  319.3 2.5 copy-start.16
  319.3 3.6 copy-start.15
Sparse Core Ops, SparseCore 0:
  289.3 15.4 all-gather.6
  306.9 32.3 all-gather.4
  340.9 32.3 all-gather.10
  374.7 32.3 all-gather.8
where the time goes:
time: 427 us; the launch traced here: 421 us
  waiting for transfers between devices  179 us (42%)
  local copies, waits for them, and re-layouts  77 us (18%)
  blocking collectives  65.6 us (15%)
  other arithmetic  61.4 us (14%)
  starting transfers between devices  20.3 us (5%)
  between operations  17.8 us (4%)
    all_to_all x4, waiting for transfers between devices, device_step(): received = lax.all_to_all(sent_grad, 'data', 2, 0, tiled=True)  111 us
    all_gather x4, waiting for transfers between devices, device_step(): lax.all_gather(new_weight.astype(jnp.bfloat16), 'data', axis=1, tiled=True)  67.4 us
    unnamed x50, local copies, waits for them, and re-layouts  66.9 us
    psum x1, blocking collectives, device_step(): total_norm = jnp.sqrt(lax.psum(local_sq, ('model', 'data')))  32.9 us
    psum x1, blocking collectives, device_step(): norm_pair = jnp.sqrt(lax.psum(sq_pair, ('model', 'data')))  32.7 us
    reduce_sum x2, other arithmetic, device_step(): jnp.sum(update * update, axis=(1, 2))  20.4 us
    all_to_all x4, starting transfers between devices, device_step(): received = lax.all_to_all(sent_grad, 'data', 2, 0, tiled=True)  19.4 us
    convert_element_type x4, other arithmetic, device_step(): new_weight.astype(jnp.bfloat16)  17.9 us
  transfers between devices with their start and end apart: 8, of which 7 were waited for; matrix products, arithmetic and copies ran while one was open for 22% of the time, Pallas kernels for 0%

commit v1 on v0

v1 whole, which is shorter than its diff:
```python
import functools

import jax
import jax.numpy as jnp
from jax import lax
from jax.experimental import pallas as pl
from jax.experimental.pallas import tpu as pltpu
from jax.sharding import PartitionSpec as P

LEARN_RATE = 0.08
BETA_ONE = 0.9
BETA_TWO = 0.999
ADAM_EPS = 1e-6
DECAY_RATE = 0.01
MAX_NORM = 1.0
STEP_COUNT = 100
COLUMN_SPLIT = (True, False, True, False)

LAYERS = 32
DATA = 4
DEVICES = 16
ROWS = (64, 16, 64, 64)
COLS = (192, 256, 256, 256)
PACK = (144, 128, 0, 64)
PACKED = 192
SLOTS = 3
AHEAD = 6
GROUP = 8
CHUNKS = 4
MESH = pl.DeviceIdType.MESH


def grad_spec(col_split):
    return P("data", None, None, "model") if col_split else P("data", None, "model", None)


def state_spec(col_split):
    return P(None, "data", "model") if col_split else P(None, ("model", "data"), None)


def replica_spec(col_split):
    return P(None, None, "model") if col_split else P(None, "model", None)


def pack_layer(dst, qkv, proj, fcin, fcout):
    dst[0:64, :] = fcin.astype(jnp.bfloat16)
    dst[64:128, :] = fcout.astype(jnp.bfloat16)
    dst[128:144, :] = proj.astype(jnp.bfloat16)
    wide = qkv[:, 0:128].astype(jnp.bfloat16)
    thin = qkv[:, 128:192]
    dst[144:176, 0:128] = wide[0:32]
    dst[144:176, 128:256] = wide[32:64]
    left = jnp.concatenate([thin[0:16], thin[16:32]], axis=1)
    right = jnp.concatenate([thin[32:48], thin[48:64]], axis=1)
    dst[176:192, 0:128] = left.astype(jnp.bfloat16)
    dst[176:192, 128:256] = right.astype(jnp.bfloat16)


def column_sums(scr):
    folded = scr[:, 0:128] + scr[:, 128:256]
    return jnp.sum(jnp.transpose(folded), axis=0, keepdims=True)


def step_kernel(*refs):
    grads, weights, firsts, seconds = refs[0:4], refs[4:8], refs[8:12], refs[12:16]
    out_w, out_m, out_v = refs[16:20], refs[20:24], refs[24:28]
    out_b = refs[28 : 28 + CHUNKS]
    scr = refs[28 + CHUNKS :]
    stage, w_buf, m_buf, v_buf, u_buf = scr[0:4], scr[4:8], scr[8:12], scr[12:16], scr[16:20]
    snd, rcv, n_acc, wn_acc, un_acc, ratio, sync_src, sync_a, sync_b = scr[20:29]
    load_sem, state_sem, send_sem, recv_sem, sync_send, sync_recv, out_sem = scr[29:36]

    d = lax.axis_index("data")
    m = lax.axis_index("model")
    gid = m * DATA + d

    def coords(dev):
        return (dev // DATA, dev % DATA)

    def loads(layer, slot):
        return [pltpu.make_async_copy(grads[a].at[0, layer], stage[a].at[slot], load_sem.at[slot, a]) for a in range(4)]

    for layer in range(SLOTS):
        for copy in loads(layer, layer):
            copy.start()

    barrier = pltpu.get_barrier_semaphore()

    def greet(off, carry):
        pl.semaphore_signal(barrier, inc=1, device_id=coords((gid + off) % DEVICES), device_id_type=MESH)
        return carry

    lax.fori_loop(1, DEVICES, greet, 0)
    pl.semaphore_wait(barrier, DEVICES - 1)

    def exchange(layer, k):
        return pltpu.make_async_remote_copy(
            src_ref=snd.at[k - 1, layer],
            dst_ref=rcv.at[k, layer],
            send_sem=send_sem.at[k - 1, layer],
            recv_sem=recv_sem.at[k - 1, layer],
            device_id=(m, (d + k) % DATA),
            device_id_type=MESH,
        )

    def produce(layer):
        slot = lax.rem(layer, SLOTS)
        for copy in loads(layer, slot):
            copy.wait()
        for k in (2, 1, 3, 0):
            owner = (d + k) % DATA
            big = pl.ds(pl.multiple_of(owner * 64, 64), 64)
            small = pl.ds(pl.multiple_of(owner * 16, 16), 16)
            dst = snd.at[k - 1, layer] if k else rcv.at[0, layer]
            pack_layer(dst, stage[0][slot, big, :], stage[1][slot, small, :], stage[2][slot, big, :], stage[3][slot, big, :])
            if k:
                exchange(layer, k).start()

        @pl.when(layer + SLOTS < LAYERS)
        def _():
            for copy in loads(layer + SLOTS, slot):
                copy.start()

    def produce_loop(layer, carry):
        produce(layer)
        return carry

    lax.fori_loop(0, AHEAD, produce_loop, 0)

    state_copies = []
    for idx, (source, target) in enumerate(((weights, w_buf), (firsts, m_buf), (seconds, v_buf))):
        for a in range(4):
            copy = pltpu.make_async_copy(source[a], target[a], state_sem.at[idx, a])
            copy.start()
            state_copies.append(copy)
    n_acc[...] = jnp.zeros_like(n_acc)
    wn_acc[...] = jnp.zeros_like(wn_acc)
    un_acc[...] = jnp.zeros_like(un_acc)
    for copy in state_copies:
        copy.wait()

    def consume(layer, carry):
        @pl.when(layer + AHEAD < LAYERS)
        def _():
            produce(layer + AHEAD)

        for a in range(4):
            w = w_buf[a][layer]
            wn_acc[pl.ds(a * LAYERS + layer, 1), 0 : COLS[a]] = jnp.sum(w * w, axis=0, keepdims=True)
        for k in (1, 2, 3):
            exchange(layer, k).wait_recv()

        def gathered(first, rows, col=0, cols=256):
            parts = [rcv[k, layer, first : first + rows, col : col + cols].astype(jnp.float32) for k in range(4)]
            return (parts[0] + parts[1] + parts[2] + parts[3]) * (1.0 / DATA)

        def squares(x):
            rows, cols = x.shape
            return jnp.sum((x * x).reshape(rows // 8, 8, cols), axis=0)

        fcin = gathered(0, 64)
        u_buf[2][layer] = fcin
        fcout = gathered(64, 64)
        u_buf[3][layer] = fcout
        proj = gathered(128, 16)
        u_buf[1][layer] = proj
        wide = gathered(144, 32)
        u_buf[0][layer, 0:32, 0:128] = wide[:, 0:128]
        u_buf[0][layer, 32:64, 0:128] = wide[:, 128:256]
        thin = gathered(176, 16)
        for q in range(4):
            u_buf[0][layer, 16 * q : 16 * q + 16, 128:192] = thin[:, 64 * q : 64 * q + 64]
        n_acc[...] += squares(fcin) + squares(fcout) + squares(proj) + squares(wide) + squares(thin)
        return carry

    lax.fori_loop(0, LAYERS, consume, 0)

    row_idx = lax.broadcasted_iota(jnp.int32, (8, 128), 0)

    def share(sync, phase, tile):
        sync_src[phase] = tile
        sync[pl.ds(gid, 1)] = tile[None]

        def tile_copy(slot, dev):
            return pltpu.make_async_remote_copy(
                src_ref=sync_src.at[phase],
                dst_ref=sync.at[slot],
                send_sem=sync_send.at[phase, (dev - gid + DEVICES) % DEVICES],
                recv_sem=sync_recv.at[phase, slot],
                device_id=coords(dev),
                device_id_type=MESH,
            )

        def send(off, carry):
            tile_copy(gid, (gid + off) % DEVICES).start()
            return carry

        def receive(off, carry):
            dev = (gid + DEVICES - off) % DEVICES
            tile_copy(dev, dev).wait_recv()
            return carry

        def drain(off, carry):
            tile_copy(gid, (gid + off) % DEVICES).wait_send()
            return carry

        lax.fori_loop(1, DEVICES, send, 0)
        lax.fori_loop(1, DEVICES, receive, 0)
        lax.fori_loop(1, DEVICES, drain, 0)
        return jnp.sum(sync[...], axis=0)

    n_row = jnp.sum(n_acc[:, 0:128] + n_acc[:, 128:256], axis=0, keepdims=True)
    tile = jnp.where(row_idx == 0, n_row, jnp.where(row_idx == 1, column_sums(wn_acc), 0.0))
    totals = share(sync_a, 0, tile)
    weight_sq = totals[1:2, :]
    total_norm = jnp.sqrt(jnp.sum(totals[0:1, :], axis=1, keepdims=True))
    clip_coef = jnp.minimum(1.0, MAX_NORM / total_norm)

    def result_copy(source, target, a, group, idx):
        part = pl.ds(group * GROUP, GROUP)
        return pltpu.make_async_copy(source[a].at[part], target[a].at[part], out_sem.at[idx, a, group])

    def direction(layer, carry):
        for a in range(4):
            w = w_buf[a][layer]
            clipped = clip_coef * u_buf[a][layer]
            first = BETA_ONE * m_buf[a][layer] + (1.0 - BETA_ONE) * clipped
            second = BETA_TWO * v_buf[a][layer] + (1.0 - BETA_TWO) * clipped * clipped
            m_buf[a][layer] = first
            v_buf[a][layer] = second
            first_hat = first * (1.0 / (1.0 - BETA_ONE**STEP_COUNT))
            second_hat = second * (1.0 / (1.0 - BETA_TWO**STEP_COUNT))
            u = first_hat / (jnp.sqrt(second_hat) + ADAM_EPS) + DECAY_RATE * w
            u_buf[a][layer] = u
            un_acc[pl.ds(a * LAYERS + layer, 1), 0 : COLS[a]] = jnp.sum(u * u, axis=0, keepdims=True)

        @pl.when(lax.rem(layer, GROUP) == GROUP - 1)
        def _():
            for a in range(4):
                result_copy(m_buf, out_m, a, layer // GROUP, 0).start()
                result_copy(v_buf, out_v, a, layer // GROUP, 1).start()

        return carry

    lax.fori_loop(0, LAYERS, direction, 0)
    for k in (1, 2, 3):

        def sent(layer, carry):
            exchange(layer, k).wait_send()
            return carry

        lax.fori_loop(0, LAYERS, sent, 0)

    totals = share(sync_b, 1, jnp.where(row_idx == 0, column_sums(un_acc), 0.0))
    scaled = LEARN_RATE * (jnp.sqrt(weight_sq) / jnp.sqrt(totals[0:1, :]))
    spread = jnp.transpose(jnp.broadcast_to(scaled, (128, 128)))
    ratio[:, 0:128] = spread
    ratio[:, 128:256] = spread

    per_chunk = LAYERS // CHUNKS

    def replica_copy(group):
        return pltpu.make_async_copy(snd.at[0, pl.ds(group * per_chunk, per_chunk)], out_b[group], out_sem.at[3, 0, group])

    for group in range(CHUNKS):

        def finish(layer, carry):
            rows = []
            for a in range(4):
                factor = ratio[pl.ds(a * LAYERS + layer, 1), 0 : COLS[a]]
                w = w_buf[a][layer] - factor * u_buf[a][layer]
                w_buf[a][layer] = w
                rows.append(w)
            pack_layer(snd.at[0, layer], *rows)
            return carry

        lax.fori_loop(group * per_chunk, (group + 1) * per_chunk, finish, 0)
        replica_copy(group).start()
        for a in range(4):
            result_copy(w_buf, out_w, a, group, 2).start()

    for group in range(CHUNKS):
        replica_copy(group).wait()
        for a in range(4):
            result_copy(m_buf, out_m, a, group, 0).wait()
            result_copy(v_buf, out_v, a, group, 1).wait()
            result_copy(w_buf, out_w, a, group, 2).wait()


def run_step(arrays):
    grads, weights, firsts, seconds = (arrays[i::4] for i in range(4))
    state_shapes = [jax.ShapeDtypeStruct(w.shape, jnp.float32) for w in weights]
    pieces = [jax.ShapeDtypeStruct((LAYERS // CHUNKS, PACKED, 256), jnp.bfloat16)] * CHUNKS
    state_scratch = [pltpu.VMEM((LAYERS, ROWS[a], COLS[a]), jnp.float32) for a in range(4)]
    scratch = [pltpu.VMEM((SLOTS, g.shape[2], g.shape[3]), jnp.float32) for g in grads]
    scratch += state_scratch * 4
    scratch += [
        pltpu.VMEM((3, LAYERS, PACKED, 256), jnp.bfloat16),
        pltpu.VMEM((4, LAYERS, PACKED, 256), jnp.bfloat16),
        pltpu.VMEM((8, 256), jnp.float32),
        pltpu.VMEM((128, 256), jnp.float32),
        pltpu.VMEM((128, 256), jnp.float32),
        pltpu.VMEM((128, 256), jnp.float32),
        pltpu.VMEM((2, 8, 128), jnp.float32),
        pltpu.VMEM((DEVICES, 8, 128), jnp.float32),
        pltpu.VMEM((DEVICES, 8, 128), jnp.float32),
        pltpu.SemaphoreType.DMA((SLOTS, 4)),
        pltpu.SemaphoreType.DMA((3, 4)),
        pltpu.SemaphoreType.DMA((3, LAYERS)),
        pltpu.SemaphoreType.DMA((3, LAYERS)),
        pltpu.SemaphoreType.DMA((2, DEVICES)),
        pltpu.SemaphoreType.DMA((2, DEVICES)),
        pltpu.SemaphoreType.DMA((4, 4, LAYERS // GROUP)),
    ]
    anywhere = pl.BlockSpec(memory_space=pl.ANY)
    return pl.pallas_call(
        step_kernel,
        out_shape=state_shapes * 3 + pieces,
        in_specs=[anywhere] * 16,
        out_specs=[anywhere] * (12 + CHUNKS),
        scratch_shapes=scratch,
        compiler_params=pltpu.CompilerParams(collective_id=0, has_side_effects=True, vmem_limit_bytes=63 << 20),
        name="lamb_step",
    )(*grads, *weights, *firsts, *seconds)


def assemble_kernel(has_alias, *refs):
    shards = refs[0:4]
    qkv, proj, fcin, fcout = refs[4 + 4 * has_alias :]
    d = lax.axis_index("data")
    partner = d + 1 - 2 * (d % 2)
    owners = (d, (d + 2) % DATA, partner, (partner + 2) % DATA)
    for owner, shard in zip(owners, shards):
        big = pl.ds(pl.multiple_of(owner * 64, 64), 64)
        small = pl.ds(pl.multiple_of(owner * 16, 16), 16)
        fcin[:, big, :] = shard[:, 0:64, :]
        fcout[:, big, :] = shard[:, 64:128, :]
        proj[:, small, :] = shard[:, 128:144, :]
        for half in range(2):
            rows = pl.ds(pl.multiple_of(owner * 64 + 32 * half, 32), 32)
            qkv[:, rows, 0:128] = shard[:, 144:176, 128 * half : 128 * half + 128]
        for q in range(4):
            rows = pl.ds(pl.multiple_of(owner * 64 + 16 * q, 16), 16)
            qkv[:, rows, 128:192] = shard[:, 176:192, 64 * q : 64 * q + 64]


def assemble(chunk, shards, previous):
    block = 2
    per_chunk = LAYERS // CHUNKS
    shapes = [(LAYERS, 256, 192), (LAYERS, 64, 256), (LAYERS, 256, 256), (LAYERS, 256, 256)]
    first = chunk * per_chunk // block
    in_specs = [pl.BlockSpec((block, PACKED, 256), lambda i: (i, 0, 0))] * 4
    in_specs += [pl.BlockSpec(memory_space=pl.ANY)] * len(previous)
    return pl.pallas_call(
        functools.partial(assemble_kernel, bool(previous)),
        grid=(per_chunk // block,),
        out_shape=[jax.ShapeDtypeStruct(s, jnp.bfloat16) for s in shapes],
        in_specs=in_specs,
        out_specs=[pl.BlockSpec((block, s[1], s[2]), lambda i: (first + i, 0, 0)) for s in shapes],
        input_output_aliases={4 + i: i for i in range(len(previous))},
        cost_estimate=pl.CostEstimate(flops=4_000_000, bytes_accessed=6_000_000, transcendentals=0),
        compiler_params=pltpu.CompilerParams(vmem_limit_bytes=16 << 20),
        name="assemble",
    )(*shards, *previous)


def solution(mesh):
    in_specs = []
    for col_split in COLUMN_SPLIT:
        in_specs.extend([grad_spec(col_split), state_spec(col_split), state_spec(col_split), state_spec(col_split)])
    out_specs = tuple([replica_spec(col_split) for col_split in COLUMN_SPLIT] + [state_spec(col_split) for col_split in COLUMN_SPLIT] * 3)

    across = [(i, (i + 2) % DATA) for i in range(DATA)]
    on_chip = [(i, i + 1 - 2 * (i % 2)) for i in range(DATA)]

    def device_step(*arrays):
        results = run_step(arrays)
        states, pieces = results[:12], results[12:]
        replicas = ()
        for chunk, own in enumerate(pieces):
            far = lax.ppermute(own, "data", across)
            near = lax.ppermute(own, "data", on_chip)
            far_near = lax.ppermute(far, "data", on_chip)
            replicas = assemble(chunk, (own, far, near, far_near), tuple(replicas))
        return tuple(replicas) + tuple(states)

    return jax.shard_map(device_step, mesh=mesh, in_specs=tuple(in_specs), out_specs=out_specs, check_vma=False)
```

time: 427 us -> 283 us (0.66); the launches traced: 421 us -> 283 us
  Pallas kernels: 0 us -> 172 us
  waiting for transfers between devices: 179 us -> 64.5 us
  blocking collectives: 65.6 us -> 0 us
  other arithmetic: 61.4 us -> 0 us
  local copies, waits for them, and re-layouts: 77 us -> 38.9 us
  between operations: 17.8 us -> 0.72 us
  starting transfers between devices: 20.3 us -> 6.11 us
    pallas_call x0 -> x5, Pallas kernels: none -> 172 us  [the longest x1 164 us: run_step(): pl.pallas_call(step_kernel, out_shape=state_shapes * 3 + pieces, in_specs...]
    all_to_all x4 -> x0, waiting for transfers between devices: 111 us -> none  [device_step(): received = lax.all_to_all(sent_grad, 'data', 2, 0, tiled=True)]
    all_gather x4 -> x0, waiting for transfers between devices: 67.4 us -> none  [device_step(): lax.all_gather(new_weight.astype(jnp.bfloat16), 'data', axis=1, tiled=True)]
    psum x2 -> x0, blocking collectives: 65.6 us -> none  [the longest x1 32.9 us: device_step(): total_norm = jnp.sqrt(lax.psum(local_sq, ('model', 'data')))]
    ppermute x0 -> x12, waiting for transfers between devices: none -> 64.5 us  [the longest x4 64.5 us: device_step(): far = lax.ppermute(own, 'data', across)]
    reduce_sum x14 -> x0, other arithmetic: 40.2 us -> none  [the longest x2 20.4 us: device_step(): jnp.sum(update * update, axis=(1, 2))]
    unnamed x50 -> x48, local copies, waits for them, and re-layouts: 66.9 us -> 38.9 us
    convert_element_type x5 -> x0, other arithmetic: 21.1 us -> none  [the longest x4 17.9 us: device_step(): new_weight.astype(jnp.bfloat16)]
  transfers between devices with their start and end apart: 8 -> 12, of which waited for: 7 -> 4; matrix products, arithmetic and copies ran while one was open for 22% -> 0% of each run, Pallas kernels for 0% -> 2%
where the time goes in v1:
time: 283 us
  Pallas kernels  172 us (61%)
  waiting for transfers between devices  64.5 us (23%)
  local copies, waits for them, and re-layouts  38.9 us (14%)
  starting transfers between devices  6.11 us (2%)
    pallas_call x1, Pallas kernels, run_step(): pl.pallas_call(step_kernel, out_shape=state_shapes * 3 + pieces, in_specs...  164 us
    ppermute x4, waiting for transfers between devices, device_step(): far = lax.ppermute(own, 'data', across)  64.5 us
    unnamed x48, local copies, waits for them, and re-layouts  38.9 us
    pallas_call x4, Pallas kernels, assemble(): pl.pallas_call(functools.partial(assemble_kernel, bool(previous)), grid=(...  8 us
  transfers between devices with their start and end apart: 12, of which 4 were waited for; matrix products, arithmetic and copies ran while one was open for 0% of the time, Pallas kernels for 2%

profile of v1, /device:TPU:0, one launch (start us, length us, event | category | flops | bytes accessed | tf_op | source)
XLA Modules:
  0.0 282.8 jit_solution(799006148361071363)
XLA Ops:
  0.6 8.3 %copy.44.refs_0_ = f32[1,32,256,192]{3,2,1,0:T(8,128)} copy(f32[1,32,256,192]{2,3,1,0:T(8,128)} %param.16) | data formatting | bytes 12582912 | tf_op args[0]
  9.0 164.5 %lamb_step.1 = (f32[32,64,192]{2,1,0:T(8,128)}, f32[32,16,256]{2,1,0:T(8,128)}, f32[32,64,256]{2,1,0:T(8,128)}, f32[32,64,256]{2,1,0:T(8,128)}, f32[32,64,192]{2...) custom-call(f32[1,32,256,192]{3,2,1,0:T(8,128)} %copy.44.refs_0_, ...), custom_call_target="tpu_custom_call" | custom-call | tf_op jit(solution)/shard_map/lamb_step/pallas_call | solution.py:316
  173.4 0.0 copy-start.3
  173.5 1.4 collective-permute-start.9
  174.9 0.0 collective-permute-start.10
  174.9 0.6 collective-permute-start.6
  175.5 0.2 collective-permute-start.7
  175.8 1.4 collective-permute-start.3
  177.1 16.8 %collective-permute-done.9.refs_1_ = bf16[8,192,256]{2,1,0:T(8,128)(2,1)S(1)} collective-permute-done((bf16[8,192,256]{2,1,0:T(8,128)(2,1)}, bf16[8,192,256]{2,1,0:T(8,128)(2,1)S(1)}, u32[]{:S(2)}, u32[]{:S(2)}) %collective-permute-start.9) | collective-permute-done | bytes 786464 | tf_op jit(solution)/shard_map/ppermute | solution.py:381
  193.9 1.4 collective-permute-start
  195.3 0.0 collective-permute-done.10.refs_2_
  195.3 0.0 collective-permute-start.11
  195.3 15.4 %collective-permute-done.6.refs_1_ = bf16[8,192,256]{2,1,0:T(8,128)(2,1)S(1)} collective-permute-done((bf16[8,192,256]{2,1,0:T(8,128)(2,1)}, bf16[8,192,256]{2,1,0:T(8,128)(2,1)S(1)}, u32[]{:S(2)}, u32[]{:S(2)}) %collective-permute-start.6) | collective-permute-done | bytes 786464 | tf_op jit(solution)/shard_map/ppermute | solution.py:381
  210.8 0.0 collective-permute-start.8
  210.8 0.0 collective-permute-done.7.refs_2_
  210.8 0.5 collective-permute-start.4
  211.3 16.3 %collective-permute-done.3.refs_1_ = bf16[8,192,256]{2,1,0:T(8,128)(2,1)S(1)} collective-permute-done((bf16[8,192,256]{2,1,0:T(8,128)(2,1)}, bf16[8,192,256]{2,1,0:T(8,128)(2,1)S(1)}, u32[]{:S(2)}, u32[]{:S(2)}) %collective-permute-start.3) | collective-permute-done | bytes 786464 | tf_op jit(solution)/shard_map/ppermute | solution.py:381
  227.6 0.0 collective-permute-start.5
  227.6 16.0 %collective-permute-done.refs_1_ = bf16[8,192,256]{2,1,0:T(8,128)(2,1)S(1)} collective-permute-done((bf16[8,192,256]{2,1,0:T(8,128)(2,1)}, bf16[8,192,256]{2,1,0:T(8,128)(2,1)S(1)}, u32[]{:S(2)}, u32[]{:S(2)}) %collective-permute-start) | collective-permute-done | bytes 786464 | tf_op jit(solution)/shard_map/ppermute | solution.py:381
  243.6 0.0 collective-permute-start.1
  243.6 0.0 collective-permute-done.11.refs_3_
  243.6 0.5 collective-permute-start.2
  244.1 0.0 copy-start.4
  244.1 1.1 copy-done.4
  245.3 2.0 assemble.4
  247.2 0.0 collective-permute-done.8.refs_3_
  247.2 0.0 copy-done.3
  247.2 0.0 copy-start.2
  247.2 2.0 assemble.5
  249.2 0.0 collective-permute-done.4.refs_2_
  249.2 0.0 collective-permute-done.5.refs_3_
  249.2 0.0 copy-done.2
  249.2 0.0 copy-start.1
  249.3 2.0 assemble.6
  251.3 0.0 collective-permute-done.1.refs_2_
  251.3 0.0 collective-permute-done.2.refs_3_
  251.3 0.0 copy-done.1
  251.3 2.0 assemble.7
  253.3 2.0 copy-done
  255.3 6.3 %copy.45 = bf16[32,256,192]{1,2,0:T(8,128)(2,1)} copy(bf16[32,256,192]{2,1,0:T(8,128)(2,1)} %copy-done) | data formatting | bytes 6291456
  261.6 0.0 copy-done.13
  261.6 1.3 copy.70
  262.9 0.0 copy-done.16
  262.9 0.8 copy.71
  263.7 0.5 copy-done.12
  264.3 1.3 copy.72
  265.6 1.0 copy-done.11
  266.6 1.3 copy.73
  267.9 1.0 copy-done.10
  269.0 1.3 copy.74
  270.3 0.1 copy-done.15
  270.3 0.8 copy.75
  271.1 0.5 copy-done.9
  271.7 1.3 copy.76
  273.0 1.0 copy-done.8
  274.0 1.3 copy.77
  275.4 1.0 copy-done.7
  276.4 1.3 copy.78
  277.7 0.1 copy-done.14
  277.8 0.8 copy.79
  278.5 0.5 copy-done.6
  279.1 1.3 copy.80
  280.4 1.0 copy-done.5
  281.4 1.3 copy.81
  (13 shorter events, 0.0 us)
Async XLA Ops:
  173.4 73.8 %copy-start.3 = (bf16[8,192,256]{2,1,0:T(8,128)(2,1)S(1)}, bf16[8,192,256]{2,1,0:T(8,128)(2,1)}, u32[]{:S(2)}) copy-start(bf16[8,192,256]{2,1,0:T(8,128)(2,1)} %get-tuple-element.50.refs_0_) | copy-start | bytes 2359300
  173.5 20.5 %collective-permute-start.9 = (bf16[8,192,256]{2,1,0:T(8,128)(2,1)}, bf16[8,192,256]{2,1,0:T(8,128)(2,1)S(1)}, u32[]{:S(2)}, u32[]{:S(2)}) collective-permute-start(bf16[8,192,256]{2,1,0:T(8,128)(2,1)} %get-tuple-element.51.refs_0_), channel_id=1, source_target_pairs={{0,2},{1,3},{2,0},{3,1},{4,6},{5,7},{6,4},{7,5},{8,10},{9,11},{10,... | collective-permute-start | bytes 2359304 | tf_op jit(solution)/shard_map/ppermute | solution.py:381
  174.9 20.4 %collective-permute-start.10 = (bf16[8,192,256]{2,1,0:T(8,128)(2,1)}, bf16[8,192,256]{2,1,0:T(8,128)(2,1)S(1)}, u32[]{:S(2)}, u32[]{:S(2)}) collective-permute-start(bf16[8,192,256]{2,1,0:T(8,128)(2,1)} %get-tuple-element.51.refs_0_), channel_id=1, source_target_pairs={{0,1},{1,0},{2,3},{3,2},{4,5},{5,4},{6,7},{7,6},{8,9},{9,8},{10,11... | collective-permute-start | bytes 2359304 | tf_op jit(solution)/shard_map/ppermute | solution.py:382
  174.9 35.9 %collective-permute-start.6 = (bf16[8,192,256]{2,1,0:T(8,128)(2,1)}, bf16[8,192,256]{2,1,0:T(8,128)(2,1)S(1)}, u32[]{:S(2)}, u32[]{:S(2)}) collective-permute-start(bf16[8,192,256]{2,1,0:T(8,128)(2,1)} %get-tuple-element.50.refs_0_), channel_id=1, source_target_pairs={{0,2},{1,3},{2,0},{3,1},{4,6},{5,7},{6,4},{7,5},{8,10},{9,11},{10,... | collective-permute-start | bytes 2359304 | tf_op jit(solution)/shard_map/ppermute | solution.py:381
  175.5 35.2 %collective-permute-start.7 = (bf16[8,192,256]{2,1,0:T(8,128)(2,1)}, bf16[8,192,256]{2,1,0:T(8,128)(2,1)S(1)}, u32[]{:S(2)}, u32[]{:S(2)}) collective-permute-start(bf16[8,192,256]{2,1,0:T(8,128)(2,1)} %get-tuple-element.50.refs_0_), channel_id=1, source_target_pairs={{0,1},{1,0},{2,3},{3,2},{4,5},{5,4},{6,7},{7,6},{8,9},{9,8},{10,11... | collective-permute-start | bytes 2359304 | tf_op jit(solution)/shard_map/ppermute | solution.py:382
  175.8 51.9 %collective-permute-start.3 = (bf16[8,192,256]{2,1,0:T(8,128)(2,1)}, bf16[8,192,256]{2,1,0:T(8,128)(2,1)S(1)}, u32[]{:S(2)}, u32[]{:S(2)}) collective-permute-start(bf16[8,192,256]{2,1,0:T(8,128)(2,1)} %get-tuple-element.49.refs_0_), channel_id=1, source_target_pairs={{0,2},{1,3},{2,0},{3,1},{4,6},{5,7},{6,4},{7,5},{8,10},{9,11},{10,... | collective-permute-start | bytes 2359304 | tf_op jit(solution)/shard_map/ppermute | solution.py:381
  193.9 49.7 %collective-permute-start = (bf16[8,192,256]{2,1,0:T(8,128)(2,1)}, bf16[8,192,256]{2,1,0:T(8,128)(2,1)S(1)}, u32[]{:S(2)}, u32[]{:S(2)}) collective-permute-start(bf16[8,192,256]{2,1,0:T(8,128)(2,1)} %get-tuple-element.48.refs_0_), channel_id=1, source_target_pairs={{0,2},{1,3},{2,0},{3,1},{4,6},{5,7},{6,4},{7,5},{8,10},{9,11},{10,... | collective-permute-start | bytes 2359304 | tf_op jit(solution)/shard_map/ppermute | solution.py:381
  195.3 48.3 %collective-permute-start.11 = (bf16[8,192,256]{2,1,0:T(8,128)(2,1)S(1)}, bf16[8,192,256]{2,1,0:T(8,128)(2,1)S(1)}, u32[]{:S(2)}, u32[]{:S(2)}) collective-permute-start(bf16[8,192,256]{2,1,0:T(8,128)(2,1)S(1)} %collective-permute-done.9.refs_1_), channel_id=1, source_target_pairs={{0,1},{1,0},{2,3},{3,2},{4,5},{5,4},{6,7},{7,6},{8,9},{9,8},{10,11... | collective-permute-start | bytes 2359304 | tf_op jit(solution)/shard_map/ppermute | solution.py:383
  210.8 36.5 %collective-permute-start.8 = (bf16[8,192,256]{2,1,0:T(8,128)(2,1)S(1)}, bf16[8,192,256]{2,1,0:T(8,128)(2,1)S(1)}, u32[]{:S(2)}, u32[]{:S(2)}) collective-permute-start(bf16[8,192,256]{2,1,0:T(8,128)(2,1)S(1)} %collective-permute-done.6.refs_1_), channel_id=1, source_target_pairs={{0,1},{1,0},{2,3},{3,2},{4,5},{5,4},{6,7},{7,6},{8,9},{9,8},{10,11... | collective-permute-start | bytes 2359304 | tf_op jit(solution)/shard_map/ppermute | solution.py:383
  210.8 38.5 %collective-permute-start.4 = (bf16[8,192,256]{2,1,0:T(8,128)(2,1)}, bf16[8,192,256]{2,1,0:T(8,128)(2,1)S(1)}, u32[]{:S(2)}, u32[]{:S(2)}) collective-permute-start(bf16[8,192,256]{2,1,0:T(8,128)(2,1)} %get-tuple-element.49.refs_0_), channel_id=1, source_target_pairs={{0,1},{1,0},{2,3},{3,2},{4,5},{5,4},{6,7},{7,6},{8,9},{9,8},{10,11... | collective-permute-start | bytes 2359304 | tf_op jit(solution)/shard_map/ppermute | solution.py:382
  227.6 21.6 %collective-permute-start.5 = (bf16[8,192,256]{2,1,0:T(8,128)(2,1)S(1)}, bf16[8,192,256]{2,1,0:T(8,128)(2,1)S(1)}, u32[]{:S(2)}, u32[]{:S(2)}) collective-permute-start(bf16[8,192,256]{2,1,0:T(8,128)(2,1)S(1)} %collective-permute-done.3.refs_1_), channel_id=1, source_target_pairs={{0,1},{1,0},{2,3},{3,2},{4,5},{5,4},{6,7},{7,6},{8,9},{9,8},{10,11... | collective-permute-start | bytes 2359304 | tf_op jit(solution)/shard_map/ppermute | solution.py:383
  243.6 7.7 %collective-permute-start.1 = (bf16[8,192,256]{2,1,0:T(8,128)(2,1)}, bf16[8,192,256]{2,1,0:T(8,128)(2,1)S(1)}, u32[]{:S(2)}, u32[]{:S(2)}) collective-permute-start(bf16[8,192,256]{2,1,0:T(8,128)(2,1)} %get-tuple-element.48.refs_0_), channel_id=1, source_target_pairs={{0,1},{1,0},{2,3},{3,2},{4,5},{5,4},{6,7},{7,6},{8,9},{9,8},{10,11... | collective-permute-start | bytes 2359304 | tf_op jit(solution)/shard_map/ppermute | solution.py:382
  243.6 7.7 %collective-permute-start.2 = (bf16[8,192,256]{2,1,0:T(8,128)(2,1)S(1)}, bf16[8,192,256]{2,1,0:T(8,128)(2,1)S(1)}, u32[]{:S(2)}, u32[]{:S(2)}) collective-permute-start(bf16[8,192,256]{2,1,0:T(8,128)(2,1)S(1)} %collective-permute-done.refs_1_), channel_id=1, source_target_pairs={{0,1},{1,0},{2,3},{3,2},{4,5},{5,4},{6,7},{7,6},{8,9},{9,8},{10,11... | collective-permute-start | bytes 2359304 | tf_op jit(solution)/shard_map/ppermute | solution.py:383
  244.1 1.1 copy-start.4
  247.2 2.0 copy-start.2
  249.2 2.0 copy-start.1
  253.3 2.0 copy-start
  255.3 6.3 %copy-start.13 = (f32[32,64,192]{2,1,0:T(8,128)S(1)}, f32[32,64,192]{2,1,0:T(8,128)}, u32[]{:S(2)}) copy-start(f32[32,64,192]{2,1,0:T(8,128)} %get-tuple-element.116) | copy-start | bytes 4718596
  261.6 1.4 copy-start.16
  261.6 2.7 copy-start.12
  264.3 2.3 copy-start.11
  266.6 2.3 copy-start.10
  269.0 1.4 copy-start.15
  269.0 2.7 copy-start.9
  271.7 2.3 copy-start.8
  274.0 2.3 copy-start.7
  276.4 1.4 copy-start.14
  276.4 2.7 copy-start.6
  279.1 2.3 copy-start.5

commit v2 on v1

v2 whole, which is shorter than its diff:
```python
import functools

import jax
import jax.numpy as jnp
from jax import lax
from jax.experimental import pallas as pl
from jax.experimental.pallas import tpu as pltpu
from jax.sharding import PartitionSpec as P


LEARN_RATE = 0.08
BETA_ONE = 0.9
BETA_TWO = 0.999
ADAM_EPS = 1e-6
DECAY_RATE = 0.01
MAX_NORM = 1.0
STEP_COUNT = 100
COLUMN_SPLIT = (True, False, True, False)

LAYERS = 32
DATA = 4
DEVICES = 16
ROWS = (64, 16, 64, 64)
COLS = (192, 256, 256, 256)
PACKED = 192
SLOTS = 3
AHEAD = 6
GROUP = 8
CHUNKS = (4, 10, 10, 6, 2)
HEAD = CHUNKS[0]
UPDATE_FLOPS = 2_000_000_000
ASSEMBLE_FLOPS = 40_000_000
FIRST_SCALE = 1.0 / (1.0 - BETA_ONE**STEP_COUNT)
SECOND_SCALE = 1.0 / (1.0 - BETA_TWO**STEP_COUNT)
MESH = pl.DeviceIdType.MESH


def grad_spec(col_split):
    return P("data", None, None, "model") if col_split else P("data", None, "model", None)


def state_spec(col_split):
    return P(None, "data", "model") if col_split else P(None, ("model", "data"), None)


def replica_spec(col_split):
    return P(None, None, "model") if col_split else P(None, "model", None)


def pack_rest(dst, proj, fcin, fcout):
    dst[0:64, :] = fcin.astype(jnp.bfloat16)
    dst[64:128, :] = fcout.astype(jnp.bfloat16)
    dst[128:144, :] = proj.astype(jnp.bfloat16)


def pack_grad(dst, qkv):
    wide = qkv[:, 0:128].astype(jnp.bfloat16)
    thin = qkv[:, 128:192]
    dst[144:176, 0:128] = wide[0:32]
    dst[144:176, 128:256] = wide[32:64]
    left = jnp.concatenate([thin[0:16], thin[16:32]], axis=1)
    right = jnp.concatenate([thin[32:48], thin[48:64]], axis=1)
    dst[176:192, 0:128] = left.astype(jnp.bfloat16)
    dst[176:192, 128:256] = right.astype(jnp.bfloat16)


def pack_turned(dst, qkv):
    turned = jnp.transpose(qkv)
    left = jnp.concatenate([turned[0:48], turned[96:144]], axis=1)
    right = jnp.concatenate([turned[48:96], turned[144:192]], axis=1)
    dst[144:192, 0:128] = left.astype(jnp.bfloat16)
    dst[144:192, 128:256] = right.astype(jnp.bfloat16)


def column_sums(scr):
    folded = scr[:, 0:128] + scr[:, 128:256]
    return jnp.sum(jnp.transpose(folded), axis=0, keepdims=True)


def step_kernel(*refs):
    grads, weights, firsts, seconds = refs[0:4], refs[4:8], refs[8:12], refs[12:16]
    out_g, out_coef, out_ratio, out_far = refs[16:20], refs[20], refs[21], refs[22]
    out_b = refs[23 : 23 + len(CHUNKS)]
    scr = refs[23 + len(CHUNKS) :]
    stage, w_buf, m_buf, v_buf, g_buf = scr[0:4], scr[4:8], scr[8:12], scr[12:16], scr[16:20]
    turned, snd, rcv, n_acc, wn_acc, un_acc, coef, ratio, sync_src, sync_buf = scr[20:30]
    load_sem, state_sem, send_sem, recv_sem, sync_send, sync_recv, far_sem, out_sem, grad_sem = scr[30:39]

    d = lax.axis_index("data")
    m = lax.axis_index("model")
    gid = m * DATA + d

    def coords(dev):
        return (dev // DATA, dev % DATA)

    def loads(layer, slot):
        return [pltpu.make_async_copy(grads[a].at[0, layer], stage[a].at[slot], load_sem.at[slot, a]) for a in range(4)]

    for layer in range(SLOTS):
        for copy in loads(layer, layer):
            copy.start()

    barrier = pltpu.get_barrier_semaphore()

    def greet(off, carry):
        pl.semaphore_signal(barrier, inc=1, device_id=coords((gid + off) % DEVICES), device_id_type=MESH)
        return carry

    lax.fori_loop(1, DEVICES, greet, 0)

    def exchange(layer, k):
        return pltpu.make_async_remote_copy(
            src_ref=snd.at[k - 1, layer],
            dst_ref=rcv.at[k, layer],
            send_sem=send_sem.at[k - 1, layer],
            recv_sem=recv_sem.at[k - 1, layer],
            device_id=(m, (d + k) % DATA),
            device_id_type=MESH,
        )

    def produce(layer, opening=False):
        slot = lax.rem(layer, SLOTS)
        for copy in loads(layer, slot):
            copy.wait()
        turned[...] = jnp.transpose(stage[0][slot])
        for k in (2, 1, 3, 0):
            owner = (d + k) % DATA
            big = pl.ds(pl.multiple_of(owner * 64, 64), 64)
            small = pl.ds(pl.multiple_of(owner * 16, 16), 16)
            dst = snd.at[k - 1, layer] if k else rcv.at[0, layer]
            pack_rest(dst, stage[1][slot, small, :], stage[2][slot, big, :], stage[3][slot, big, :])
            pack_grad(dst, turned[big, :])
            if k and not opening:
                exchange(layer, k).start()
        if opening:
            pl.semaphore_wait(barrier, DEVICES - 1)
            for k in (2, 1, 3):
                exchange(layer, k).start()

        @pl.when(layer + SLOTS < LAYERS)
        def _():
            for copy in loads(layer + SLOTS, slot):
                copy.start()

    def produce_loop(layer, carry):
        produce(layer)
        return carry

    produce(jnp.int32(0), opening=True)
    lax.fori_loop(1, AHEAD, produce_loop, 0)

    state_copies = []
    for idx, (source, target) in enumerate(((weights, w_buf), (firsts, m_buf), (seconds, v_buf))):
        for a in range(4):
            copy = pltpu.make_async_copy(source[a], target[a], state_sem.at[idx, a])
            copy.start()
            state_copies.append(copy)
    n_acc[...] = jnp.zeros_like(n_acc)
    wn_acc[...] = jnp.zeros_like(wn_acc)
    un_acc[...] = jnp.zeros_like(un_acc)
    for copy in state_copies:
        copy.wait()

    def grad_copy(a, group):
        part = pl.ds(group * GROUP, GROUP)
        return pltpu.make_async_copy(g_buf[a].at[part], out_g[a].at[part], grad_sem.at[a, group])

    def consume(layer, carry):
        @pl.when(layer + AHEAD < LAYERS)
        def _():
            produce(layer + AHEAD)

        for a in range(4):
            w = w_buf[a][layer]
            wn_acc[pl.ds(a * LAYERS + layer, 1), 0 : COLS[a]] = jnp.sum(w * w, axis=0, keepdims=True)
            m_buf[a][layer] = (BETA_ONE * FIRST_SCALE) * m_buf[a][layer]
            v_buf[a][layer] = (BETA_TWO * SECOND_SCALE) * v_buf[a][layer]
        for k in (1, 2, 3):
            exchange(layer, k).wait_recv()

        def gathered(first, rows):
            parts = [rcv[k, layer, first : first + rows, :].astype(jnp.float32) for k in range(4)]
            return (parts[0] + parts[1] + parts[2] + parts[3]) * (1.0 / DATA)

        def squares(x):
            rows, cols = x.shape
            return jnp.sum((x * x).reshape(rows // 8, 8, cols), axis=0)

        fcin = gathered(0, 64)
        g_buf[2][layer] = fcin
        fcout = gathered(64, 64)
        g_buf[3][layer] = fcout
        proj = gathered(128, 16)
        g_buf[1][layer] = proj
        wide = gathered(144, 32)
        g_buf[0][layer, 0:32, 0:128] = wide[:, 0:128]
        g_buf[0][layer, 32:64, 0:128] = wide[:, 128:256]
        thin = gathered(176, 16)
        for q in range(4):
            g_buf[0][layer, 16 * q : 16 * q + 16, 128:192] = thin[:, 64 * q : 64 * q + 64]
        n_acc[...] += squares(fcin) + squares(fcout) + squares(proj) + squares(wide) + squares(thin)

        @pl.when(lax.rem(layer, GROUP) == GROUP - 1)
        def _():
            for a in range(4):
                grad_copy(a, layer // GROUP).start()

        return carry

    lax.fori_loop(0, LAYERS, consume, 0)

    row_idx = lax.broadcasted_iota(jnp.int32, (8, 128), 0)

    def tile_copy(phase, slot, dev):
        return pltpu.make_async_remote_copy(
            src_ref=sync_src.at[phase],
            dst_ref=sync_buf.at[phase, slot],
            send_sem=sync_send.at[phase, (dev - gid + DEVICES) % DEVICES],
            recv_sem=sync_recv.at[phase, slot],
            device_id=coords(dev),
            device_id_type=MESH,
        )

    def share(phase, tile):
        sync_src[phase] = tile
        sync_buf[phase, pl.ds(gid, 1)] = tile[None]

        def send(off, carry):
            tile_copy(phase, gid, (gid + off) % DEVICES).start()
            return carry

        lax.fori_loop(1, DEVICES, send, 0)

    def collect(phase):
        def receive(off, carry):
            dev = (gid + DEVICES - off) % DEVICES
            tile_copy(phase, dev, dev).wait_recv()
            return carry

        lax.fori_loop(1, DEVICES, receive, 0)
        return jnp.sum(sync_buf[phase], axis=0)

    n_row = jnp.sum(n_acc[:, 0:128] + n_acc[:, 128:256], axis=0, keepdims=True)
    share(0, jnp.where(row_idx == 0, n_row, 0.0))
    share(1, jnp.where(row_idx == 0, column_sums(wn_acc), 0.0))
    total_norm = jnp.sqrt(jnp.sum(collect(0)[0:1, :], axis=1, keepdims=True))
    clip_coef = jnp.minimum(1.0, MAX_NORM / total_norm)
    coef[...] = jnp.broadcast_to(clip_coef, (8, 128))
    first_coef = ((1.0 - BETA_ONE) * FIRST_SCALE) * clip_coef
    second_coef = ((1.0 - BETA_TWO) * SECOND_SCALE) * clip_coef * clip_coef

    def direction(layer, carry):
        for a in range(4):
            g = g_buf[a][layer]
            first_hat = m_buf[a][layer] + first_coef * g
            second_hat = v_buf[a][layer] + second_coef * (g * g)
            u = first_hat / (jnp.sqrt(second_hat) + ADAM_EPS) + DECAY_RATE * w_buf[a][layer]
            m_buf[a][layer] = u
            un_acc[pl.ds(a * LAYERS + layer, 1), 0 : COLS[a]] = jnp.sum(u * u, axis=0, keepdims=True)
        return carry

    def set_ratio(weight_sq, update_sq):
        scaled = LEARN_RATE * (jnp.sqrt(weight_sq) / jnp.sqrt(update_sq))
        spread = jnp.transpose(jnp.broadcast_to(scaled, (128, 128)))
        ratio[:, 0:128] = spread
        ratio[:, 128:256] = spread

    def finish(layer, carry):
        rows = []
        for a in range(4):
            factor = ratio[pl.ds(a * LAYERS + layer, 1), 0 : COLS[a]]
            rows.append(w_buf[a][layer] - factor * m_buf[a][layer])
        pack_rest(snd.at[0, layer], *rows[1:])
        pack_turned(snd.at[0, layer], rows[0])
        return carry

    def sent(layer, carry):
        for k in (1, 2, 3):
            exchange(layer, k).wait_send()
        return carry

    starts = [sum(CHUNKS[:i]) for i in range(len(CHUNKS))]

    def replica_copy(i):
        return pltpu.make_async_copy(snd.at[0, pl.ds(starts[i], CHUNKS[i])], out_b[i], out_sem.at[i])

    far = pltpu.make_async_remote_copy(
        src_ref=snd.at[0, pl.ds(0, HEAD)],
        dst_ref=out_far,
        send_sem=far_sem.at[0],
        recv_sem=far_sem.at[1],
        device_id=(m, (d + 2) % DATA),
        device_id_type=MESH,
    )
    coef_copy = pltpu.make_async_copy(coef, out_coef, out_sem.at[len(CHUNKS)])
    ratio_copy = pltpu.make_async_copy(ratio, out_ratio, out_sem.at[len(CHUNKS) + 1])

    lane = lax.broadcasted_iota(jnp.int32, (1, 128), 1) % LAYERS
    lax.fori_loop(0, HEAD, direction, 0)
    share(2, jnp.where(row_idx == 0, column_sums(un_acc), 0.0))
    coef_copy.start()
    lax.fori_loop(0, LAYERS, sent, 0)
    lax.fori_loop(HEAD, LAYERS, direction, 0)
    share(3, jnp.where(row_idx == 0, column_sums(un_acc), 0.0))
    weight_sq = collect(1)[0:1, :]
    set_ratio(weight_sq, jnp.where(lane < HEAD, collect(2)[0:1, :], 1.0))
    lax.fori_loop(0, HEAD, finish, 0)
    far.start()
    replica_copy(0).start()
    set_ratio(weight_sq, collect(3)[0:1, :])
    ratio_copy.start()
    for i in range(1, len(CHUNKS)):
        lax.fori_loop(starts[i], starts[i] + CHUNKS[i], finish, 0)
        replica_copy(i).start()

    def drain(off, carry):
        for phase in range(4):
            tile_copy(phase, gid, (gid + off) % DEVICES).wait_send()
        return carry

    lax.fori_loop(1, DEVICES, drain, 0)
    coef_copy.wait()
    ratio_copy.wait()
    for group in range(LAYERS // GROUP):
        for a in range(4):
            grad_copy(a, group).wait()
    for i in range(len(CHUNKS)):
        replica_copy(i).wait()
    far.wait()


def run_step(grads, weights, firsts, seconds):
    state_shapes = [jax.ShapeDtypeStruct(w.shape, jnp.float32) for w in weights]
    pieces = [jax.ShapeDtypeStruct((n, PACKED, 256), jnp.bfloat16) for n in CHUNKS]
    small = [jax.ShapeDtypeStruct((8, 128), jnp.float32), jax.ShapeDtypeStruct((128, 256), jnp.float32)]
    state_scratch = [pltpu.VMEM((LAYERS, ROWS[a], COLS[a]), jnp.float32) for a in range(4)]
    scratch = [pltpu.VMEM((SLOTS, g.shape[2], g.shape[3]), jnp.float32) for g in grads]
    scratch += state_scratch * 4
    scratch += [
        pltpu.VMEM((256, 192), jnp.float32),
        pltpu.VMEM((3, LAYERS, PACKED, 256), jnp.bfloat16),
        pltpu.VMEM((4, LAYERS, PACKED, 256), jnp.bfloat16),
        pltpu.VMEM((8, 256), jnp.float32),
        pltpu.VMEM((128, 256), jnp.float32),
        pltpu.VMEM((128, 256), jnp.float32),
        pltpu.VMEM((8, 128), jnp.float32),
        pltpu.VMEM((128, 256), jnp.float32),
        pltpu.VMEM((4, 8, 128), jnp.float32),
        pltpu.VMEM((4, DEVICES, 8, 128), jnp.float32),
        pltpu.SemaphoreType.DMA((SLOTS, 4)),
        pltpu.SemaphoreType.DMA((3, 4)),
        pltpu.SemaphoreType.DMA((3, LAYERS)),
        pltpu.SemaphoreType.DMA((3, LAYERS)),
        pltpu.SemaphoreType.DMA((4, DEVICES)),
        pltpu.SemaphoreType.DMA((4, DEVICES)),
        pltpu.SemaphoreType.DMA((2,)),
        pltpu.SemaphoreType.DMA((len(CHUNKS) + 2,)),
        pltpu.SemaphoreType.DMA((4, LAYERS // GROUP)),
    ]
    anywhere = pl.BlockSpec(memory_space=pl.ANY)
    out_shape = state_shapes + small + pieces[:1] + pieces
    results = pl.pallas_call(
        step_kernel,
        out_shape=out_shape,
        in_specs=[anywhere] * 16,
        out_specs=[anywhere] * len(out_shape),
        scratch_shapes=scratch,
        compiler_params=pltpu.CompilerParams(collective_id=0, has_side_effects=True, vmem_limit_bytes=63 << 20),
        name="lamb_step",
    )(*grads, *weights, *firsts, *seconds)
    return results[0:4], results[4], results[5], results[6], results[7:]


def update_kernel(*refs):
    coef, ratio = refs[0], refs[1]
    means, weights, firsts, seconds = refs[2:6], refs[6:10], refs[10:14], refs[14:18]
    out_w, out_m, out_v = refs[18:22], refs[22:26], refs[26:30]
    clip_coef = coef[0:1, 0:1]
    block = means[0].shape[0]
    for b in range(block):
        layer = pl.program_id(0) * block + b
        for a in range(4):
            w = weights[a][b]
            clipped = clip_coef * means[a][b]
            first = BETA_ONE * firsts[a][b] + (1.0 - BETA_ONE) * clipped
            second = BETA_TWO * seconds[a][b] + (1.0 - BETA_TWO) * clipped * clipped
            out_m[a][b] = first
            out_v[a][b] = second
            u = (first * FIRST_SCALE) / (jnp.sqrt(second * SECOND_SCALE) + ADAM_EPS) + DECAY_RATE * w
            out_w[a][b] = w - ratio[pl.ds(a * LAYERS + layer, 1), 0 : COLS[a]] * u


def update(coef, ratio, means, weights, firsts, seconds):
    block = 2
    layer_specs = [pl.BlockSpec((block, ROWS[a], COLS[a]), lambda i: (i, 0, 0)) for a in range(4)]
    return pl.pallas_call(
        update_kernel,
        grid=(LAYERS // block,),
        out_shape=[jax.ShapeDtypeStruct(w.shape, jnp.float32) for w in weights] * 3,
        in_specs=[pl.BlockSpec((8, 128), lambda i: (0, 0)), pl.BlockSpec((128, 256), lambda i: (0, 0))] + layer_specs * 4,
        out_specs=layer_specs * 3,
        cost_estimate=pl.CostEstimate(flops=UPDATE_FLOPS, bytes_accessed=47_000_000, transcendentals=0),
        compiler_params=pltpu.CompilerParams(vmem_limit_bytes=60 << 20),
        name="update",
    )(coef, ratio, *means, *weights, *firsts, *seconds)


def assemble_kernel(has_alias, *refs):
    shards = refs[0:4]
    qkv, proj, fcin, fcout, parts = refs[4 + 4 * has_alias :]
    d = lax.axis_index("data")
    partner = d + 1 - 2 * (d % 2)
    owners = (d, (d + 2) % DATA, partner, (partner + 2) % DATA)
    for owner, shard in zip(owners, shards):
        big = pl.ds(pl.multiple_of(owner * 64, 64), 64)
        small = pl.ds(pl.multiple_of(owner * 16, 16), 16)
        fcin[:, big, :] = shard[:, 0:64, :]
        fcout[:, big, :] = shard[:, 64:128, :]
        proj[:, small, :] = shard[:, 128:144, :]
        parts[owner] = shard[:, 144:192, :]
    for half in range(2):
        first, second = parts[2 * half], parts[2 * half + 1]
        for q, lane in ((0, 0), (48, 128), (96, 64), (144, 192)):
            pair = jnp.concatenate([first[:, :, lane : lane + 64], second[:, :, lane : lane + 64]], axis=2)
            qkv[:, q : q + 48, 128 * half : 128 * half + 128] = pair


def assemble(chunk, shards, previous):
    block = 2
    shapes = [(LAYERS, 192, 256), (LAYERS, 64, 256), (LAYERS, 256, 256), (LAYERS, 256, 256)]
    first = sum(CHUNKS[:chunk]) // block
    in_specs = [pl.BlockSpec((block, PACKED, 256), lambda i: (i, 0, 0))] * 4
    in_specs += [pl.BlockSpec(memory_space=pl.ANY)] * len(previous)
    return pl.pallas_call(
        functools.partial(assemble_kernel, bool(previous)),
        grid=(CHUNKS[chunk] // block,),
        out_shape=[jax.ShapeDtypeStruct(s, jnp.bfloat16) for s in shapes],
        in_specs=in_specs,
        out_specs=[pl.BlockSpec((block, s[1], s[2]), lambda i: (first + i, 0, 0)) for s in shapes],
        scratch_shapes=[pltpu.VMEM((4, block, 48, 256), jnp.bfloat16)],
        input_output_aliases={4 + i: i for i in range(len(previous))},
        cost_estimate=pl.CostEstimate(flops=ASSEMBLE_FLOPS * CHUNKS[chunk], bytes_accessed=800_000 * CHUNKS[chunk], transcendentals=0),
        compiler_params=pltpu.CompilerParams(vmem_limit_bytes=24 << 20),
        name="assemble",
    )(*shards, *previous)


def solution(mesh):
    in_specs = []
    for col_split in COLUMN_SPLIT:
        in_specs.extend([grad_spec(col_split), state_spec(col_split), state_spec(col_split), state_spec(col_split)])
    out_specs = tuple([replica_spec(col_split) for col_split in COLUMN_SPLIT] + [state_spec(col_split) for col_split in COLUMN_SPLIT] * 3)

    across = [(i, (i + 2) % DATA) for i in range(DATA)]
    on_chip = [(i, i + 1 - 2 * (i % 2)) for i in range(DATA)]

    def device_step(*arrays):
        grads, weights, firsts, seconds = (arrays[i::4] for i in range(4))
        grads = (jnp.swapaxes(grads[0], 2, 3), *grads[1:])
        means, coef, ratio, far_head, pieces = run_step(grads, weights, firsts, seconds)
        states = update(coef, ratio, means, weights, firsts, seconds)
        replicas = ()
        for chunk, own in enumerate(pieces):
            far = lax.ppermute(own, "data", across) if chunk else far_head
            near = lax.ppermute(own, "data", on_chip)
            far_near = lax.ppermute(far, "data", on_chip)
            replicas = assemble(chunk, (own, far, near, far_near), tuple(replicas))
        return (jnp.swapaxes(replicas[0], 1, 2), *replicas[1:], *states)

    return jax.shard_map(device_step, mesh=mesh, in_specs=tuple(in_specs), out_specs=out_specs, check_vma=False)
```

time: 283 us -> 279 us (0.986)
  local copies, waits for them, and re-layouts: 38.9 us -> 8.06 us
  Pallas kernels: 172 us -> 202 us
  waiting for transfers between devices: 64.5 us -> 60 us
    unnamed x48 -> x24, local copies, waits for them, and re-layouts: 38.9 us -> 8.06 us
    pallas_call x1 -> x2, Pallas kernels: 164 us -> 188 us  [the longest x1 166 us: run_step(): pl.pallas_call(step_kernel, out_shape=out_shape, in_specs=[anywhere] * 16...]
    pallas_call x4 -> x5, Pallas kernels: 8 us -> 14.6 us  [assemble(): pl.pallas_call(functools.partial(assemble_kernel, bool(previous)), grid=(...]
    ppermute x4, waiting for transfers between devices: 64.5 us -> 60 us  [device_step(): far = lax.ppermute(own, 'data', across) if chunk else far_head]
  transfers between devices with their start and end apart: 12 -> 14, of which waited for: 4 -> 2; matrix products, arithmetic and copies ran while one was open for 0% -> 0% of each run, Pallas kernels for 2% -> 12%
where the time goes in v2:
time: 279 us; the launch traced here: 278 us
  Pallas kernels  202 us (72%)
  waiting for transfers between devices  60 us (22%)
  local copies, waits for them, and re-layouts  8.06 us (3%)
  starting transfers between devices  6.43 us (2%)
    pallas_call x1, Pallas kernels, run_step(): pl.pallas_call(step_kernel, out_shape=out_shape, in_specs=[anywhere] * 16...  166 us
    ppermute x4, waiting for transfers between devices, device_step(): far = lax.ppermute(own, 'data', across) if chunk else far_head  60 us
    pallas_call x1, Pallas kernels, update(): pl.pallas_call(update_kernel, grid=(LAYERS // block,), out_shape=[jax.Sha...  21.5 us
    pallas_call x5, Pallas kernels, assemble(): pl.pallas_call(functools.partial(assemble_kernel, bool(previous)), grid=(...  14.6 us
    unnamed x24, local copies, waits for them, and re-layouts  8.06 us
  transfers between devices with their start and end apart: 14, of which 2 were waited for; matrix products, arithmetic and copies ran while one was open for 0% of the time, Pallas kernels for 12%

profile of v2, /device:TPU:0, one launch (start us, length us, event | category | flops | bytes accessed | tf_op | source)
XLA Modules:
  0.0 277.5 jit_solution(3580927334761184160)
XLA Ops:
  0.6 166.2 %lamb_step.1 = (f32[32,64,192]{2,1,0:T(8,128)}, f32[32,16,256]{2,1,0:T(8,128)}, f32[32,64,256]{2,1,0:T(8,128)}, f32[32,64,256]{2,1,0:T(8,128)}, f32[8,128]{1,0:T...) custom-call(f32[1,32,192,256]{3,2,1,0:T(8,128)} %bitcast.3, ...), custom_call_target="tpu_custom_call" | custom-call | tf_op jit(solution)/shard_map/lamb_step/pallas_call | solution.py:362
  166.8 1.1 collective-permute-start.9
  168.0 0.9 collective-permute-start.6
  168.9 1.1 collective-permute-start
  170.0 0.0 collective-permute-start.12
  170.0 0.5 collective-permute-start.13
  170.5 45.2 %collective-permute-done.refs_1_ = bf16[2,192,256]{2,1,0:T(8,128)(2,1)S(1)} collective-permute-done((bf16[2,192,256]{2,1,0:T(8,128)(2,1)}, bf16[2,192,256]{2,1,0:T(8,128)(2,1)S(1)}, u32[]{:S(2)}, u32[]{:S(2)}) %collective-permute-start) | collective-permute-done | bytes 196640 | tf_op jit(solution)/shard_map/ppermute | solution.py:464
  215.7 0.0 collective-permute-start.10
  215.7 0.0 collective-permute-done.12.refs_2_
  215.7 0.0 copy-start.7
  215.7 0.7 copy-done.7
  216.5 0.5 collective-permute-start.7
  217.0 0.0 collective-permute-done.9.refs_1_
  217.0 0.0 collective-permute-start.11
  217.0 0.0 collective-permute-done.13.refs_3_
  217.0 0.0 copy-start.9
  217.0 0.7 copy-done.9
  217.7 1.0 collective-permute-start.3
  218.7 0.0 collective-permute-done.6.refs_1_
  218.8 0.2 collective-permute-start.8
  219.0 14.8 %collective-permute-done.3.refs_1_ = bf16[6,192,256]{2,1,0:T(8,128)(2,1)} collective-permute-done((bf16[6,192,256]{2,1,0:T(8,128)(2,1)}, bf16[6,192,256]{2,1,0:T(8,128)(2,1)}, u32[]{:S(2)}, u32[]{:S(2)}) %collective-permute-start.3) | collective-permute-done | bytes 589856 | tf_op jit(solution)/shard_map/ppermute | solution.py:464
  233.8 0.0 collective-permute-start.4
  233.8 0.0 collective-permute-done.10.refs_2_
  233.8 0.5 collective-permute-start.5
  234.3 0.0 collective-permute-done.7.refs_2_
  234.3 0.0 collective-permute-start.1
  234.3 0.0 collective-permute-done.11.refs_3_
  234.3 0.0 copy-start.2
  234.3 1.0 copy-done.2
  235.3 0.5 collective-permute-start.2
  235.8 21.5 %update.1 = (f32[32,64,192]{2,1,0:T(8,128)}, f32[32,16,256]{2,1,0:T(8,128)}, f32[32,64,256]{2,1,0:T(8,128)}, f32[32,64,256]{2,1,0:T(8,128)}, f32[32,64,192]{2,1,...) custom-call(f32[8,128]{1,0:T(8,128)} %get-tuple-element.86.refs_0_, ...), custom_call_target="tpu_custom_call" | custom-call | flops 2000000000 | bytes 47000000 | tf_op jit(solution)/shard_map/update/pallas_call | solution.py:396
  257.3 0.0 copy-start.5
  257.3 1.0 copy-done.5
  258.2 0.0 copy-start.6
  258.3 1.0 copy-done.6
  259.2 0.0 copy-start.8
  259.2 1.0 copy-done.8
  260.2 0.0 copy-start.10
  260.2 1.0 copy-done.10
  261.2 0.0 copy-start.1
  261.2 1.2 assemble.5
  262.5 0.4 copy-done.1
  262.9 0.0 copy-start.3
  262.9 1.2 copy-done.3
  264.1 0.0 copy-start
  264.1 2.9 %assemble.6 = (bf16[32,192,256]{2,1,0:T(8,128)(2,1)}, bf16[32,64,256]{2,1,0:T(8,128)(2,1)}, bf16[32,256,256]{2,1,0:T(8,128)(2,1)}, bf16[32,256,256]{2,1,0:T(8,128)(2,1)}) custom-call(bf16[10,192,256]{2,1,0:T(8,128)(2,1)S(1)} %copy-done.1, ...), custom_call_target="tpu_custom_call", output_to_operand_aliasing={{0}: (4, {}), {1}: (5, {}), {2}: (6, {}), {3}: (7, {})} | custom-call | flops 400000000 | bytes 8000000 | tf_op jit(solution)/shard_map/assemble/pallas_call | solution.py:434
  267.0 0.0 collective-permute-done.8.refs_3_
  267.0 0.0 copy-done
  267.0 0.0 copy-start.4
  267.0 4.6 %assemble.7 = (bf16[32,192,256]{2,1,0:T(8,128)(2,1)}, bf16[32,64,256]{2,1,0:T(8,128)(2,1)}, bf16[32,256,256]{2,1,0:T(8,128)(2,1)}, bf16[32,256,256]{2,1,0:T(8,128)(2,1)}) custom-call(bf16[10,192,256]{2,1,0:T(8,128)(2,1)S(1)} %copy-done, ...), custom_call_target="tpu_custom_call", output_to_operand_aliasing={{0}: (4, {}), {1}: (5, {}), {2}: (6, {}), {3}: (7, {})} | custom-call | flops 400000000 | bytes 8000000 | tf_op jit(solution)/shard_map/assemble/pallas_call | solution.py:434
  271.6 0.0 collective-permute-done.4.refs_2_
  271.6 0.0 collective-permute-done.5.refs_3_
  271.6 0.0 copy-done.4
  271.6 0.0 copy-start.11
  271.7 3.9 %assemble.8 = (bf16[32,192,256]{2,1,0:T(8,128)(2,1)}, bf16[32,64,256]{2,1,0:T(8,128)(2,1)}, bf16[32,256,256]{2,1,0:T(8,128)(2,1)}, bf16[32,256,256]{2,1,0:T(8,128)(2,1)}) custom-call(bf16[6,192,256]{2,1,0:T(8,128)(2,1)S(1)} %copy-done.4, ...), custom_call_target="tpu_custom_call", output_to_operand_aliasing={{0}: (4, {}), {1}: (5, {}), {2}: (6, {}), {3}: (7, {})} | custom-call | flops 240000000 | bytes 4800000 | tf_op jit(solution)/shard_map/assemble/pallas_call | solution.py:434
  275.5 0.0 collective-permute-done.1.refs_2_
  275.5 0.0 collective-permute-done.2.refs_3_
  275.6 0.0 copy-done.11
  275.6 2.0 assemble.9
Async XLA Ops:
  166.8 50.1 %collective-permute-start.9 = (bf16[10,192,256]{2,1,0:T(8,128)(2,1)}, bf16[10,192,256]{2,1,0:T(8,128)(2,1)S(1)}, u32[]{:S(2)}, u32[]{:S(2)}) collective-permute-start(bf16[10,192,256]{2,1,0:T(8,128)(2,1)} %get-tuple-element.63.refs_0_), channel_id=1, source_target_pairs={{0,2},{1,3},{2,0},{3,1},{4,6},{5,7},{6,4},{7,5},{8,10},{9,11},{10,... | collective-permute-start | bytes 2949128 | tf_op jit(solution)/shard_map/ppermute | solution.py:464
  168.0 50.8 %collective-permute-start.6 = (bf16[10,192,256]{2,1,0:T(8,128)(2,1)}, bf16[10,192,256]{2,1,0:T(8,128)(2,1)S(1)}, u32[]{:S(2)}, u32[]{:S(2)}) collective-permute-start(bf16[10,192,256]{2,1,0:T(8,128)(2,1)} %get-tuple-element.62.refs_0_), channel_id=1, source_target_pairs={{0,2},{1,3},{2,0},{3,1},{4,6},{5,7},{6,4},{7,5},{8,10},{9,11},{10,... | collective-permute-start | bytes 2949128 | tf_op jit(solution)/shard_map/ppermute | solution.py:464
  168.9 46.8 %collective-permute-start = (bf16[2,192,256]{2,1,0:T(8,128)(2,1)}, bf16[2,192,256]{2,1,0:T(8,128)(2,1)S(1)}, u32[]{:S(2)}, u32[]{:S(2)}) collective-permute-start(bf16[2,192,256]{2,1,0:T(8,128)(2,1)} %get-tuple-element.60.refs_0_), channel_id=1, source_target_pairs={{0,2},{1,3},{2,0},{3,1},{4,6},{5,7},{6,4},{7,5},{8,10},{9,11},{10,... | collective-permute-start | bytes 589832 | tf_op jit(solution)/shard_map/ppermute | solution.py:464
  170.0 45.7 %collective-permute-start.12 = (bf16[4,192,256]{2,1,0:T(8,128)(2,1)}, bf16[4,192,256]{2,1,0:T(8,128)(2,1)S(1)}, u32[]{:S(2)}, u32[]{:S(2)}) collective-permute-start(bf16[4,192,256]{2,1,0:T(8,128)(2,1)} %get-tuple-element.64.refs_0_), channel_id=1, source_target_pairs={{0,1},{1,0},{2,3},{3,2},{4,5},{5,4},{6,7},{7,6},{8,9},{9,8},{10,11... | collective-permute-start | bytes 1179656 | tf_op jit(solution)/shard_map/ppermute | solution.py:465
  170.0 47.0 %collective-permute-start.13 = (bf16[4,192,256]{2,1,0:T(8,128)(2,1)}, bf16[4,192,256]{2,1,0:T(8,128)(2,1)S(1)}, u32[]{:S(2)}, u32[]{:S(2)}) collective-permute-start(bf16[4,192,256]{2,1,0:T(8,128)(2,1)} %get-tuple-element.65.refs_1_), channel_id=1, source_target_pairs={{0,1},{1,0},{2,3},{3,2},{4,5},{5,4},{6,7},{7,6},{8,9},{9,8},{10,11... | collective-permute-start | bytes 1179656 | tf_op jit(solution)/shard_map/ppermute | solution.py:466
  215.7 18.1 %collective-permute-start.10 = (bf16[10,192,256]{2,1,0:T(8,128)(2,1)}, bf16[10,192,256]{2,1,0:T(8,128)(2,1)S(1)}, u32[]{:S(2)}, u32[]{:S(2)}) collective-permute-start(bf16[10,192,256]{2,1,0:T(8,128)(2,1)} %get-tuple-element.63.refs_0_), channel_id=1, source_target_pairs={{0,1},{1,0},{2,3},{3,2},{4,5},{5,4},{6,7},{7,6},{8,9},{9,8},{10,11... | collective-permute-start | bytes 2949128 | tf_op jit(solution)/shard_map/ppermute | solution.py:465
  215.7 0.7 copy-start.7
  216.5 17.8 %collective-permute-start.7 = (bf16[10,192,256]{2,1,0:T(8,128)(2,1)}, bf16[10,192,256]{2,1,0:T(8,128)(2,1)S(1)}, u32[]{:S(2)}, u32[]{:S(2)}) collective-permute-start(bf16[10,192,256]{2,1,0:T(8,128)(2,1)} %get-tuple-element.62.refs_0_), channel_id=1, source_target_pairs={{0,1},{1,0},{2,3},{3,2},{4,5},{5,4},{6,7},{7,6},{8,9},{9,8},{10,11... | collective-permute-start | bytes 2949128 | tf_op jit(solution)/shard_map/ppermute | solution.py:465
  217.0 17.4 %collective-permute-start.11 = (bf16[10,192,256]{2,1,0:T(8,128)(2,1)S(1)}, bf16[10,192,256]{2,1,0:T(8,128)(2,1)S(1)}, u32[]{:S(2)}, u32[]{:S(2)}) collective-permute-start(bf16[10,192,256]{2,1,0:T(8,128)(2,1)S(1)} %collective-permute-done.9.refs_1_), channel_id=1, source_target_pairs={{0,1},{1,0},{2,3},{3,2},{4,5},{5,4},{6,7},{7,6},{8,9},{9,8},{10,11... | collective-permute-start | bytes 2949128 | tf_op jit(solution)/shard_map/ppermute | solution.py:466
  217.0 0.7 copy-start.9
  217.7 16.1 %collective-permute-start.3 = (bf16[6,192,256]{2,1,0:T(8,128)(2,1)}, bf16[6,192,256]{2,1,0:T(8,128)(2,1)}, u32[]{:S(2)}, u32[]{:S(2)}) collective-permute-start(bf16[6,192,256]{2,1,0:T(8,128)(2,1)} %get-tuple-element.61.refs_0_), channel_id=1, source_target_pairs={{0,2},{1,3},{2,0},{3,1},{4,6},{5,7},{6,4},{7,5},{8,10},{9,11},{10,... | collective-permute-start | bytes 1769480 | tf_op jit(solution)/shard_map/ppermute | solution.py:464
  218.8 48.3 %collective-permute-start.8 = (bf16[10,192,256]{2,1,0:T(8,128)(2,1)S(1)}, bf16[10,192,256]{2,1,0:T(8,128)(2,1)}, u32[]{:S(2)}, u32[]{:S(2)}) collective-permute-start(bf16[10,192,256]{2,1,0:T(8,128)(2,1)S(1)} %collective-permute-done.6.refs_1_), channel_id=1, source_target_pairs={{0,1},{1,0},{2,3},{3,2},{4,5},{5,4},{6,7},{7,6},{8,9},{9,8},{10,11... | collective-permute-start | bytes 2949128 | tf_op jit(solution)/shard_map/ppermute | solution.py:466
  233.8 37.8 %collective-permute-start.4 = (bf16[6,192,256]{2,1,0:T(8,128)(2,1)}, bf16[6,192,256]{2,1,0:T(8,128)(2,1)}, u32[]{:S(2)}, u32[]{:S(2)}) collective-permute-start(bf16[6,192,256]{2,1,0:T(8,128)(2,1)} %get-tuple-element.61.refs_0_), channel_id=1, source_target_pairs={{0,1},{1,0},{2,3},{3,2},{4,5},{5,4},{6,7},{7,6},{8,9},{9,8},{10,11... | collective-permute-start | bytes 1769480 | tf_op jit(solution)/shard_map/ppermute | solution.py:465
  233.8 37.8 %collective-permute-start.5 = (bf16[6,192,256]{2,1,0:T(8,128)(2,1)}, bf16[6,192,256]{2,1,0:T(8,128)(2,1)}, u32[]{:S(2)}, u32[]{:S(2)}) collective-permute-start(bf16[6,192,256]{2,1,0:T(8,128)(2,1)} %collective-permute-done.3.refs_1_), channel_id=1, source_target_pairs={{0,1},{1,0},{2,3},{3,2},{4,5},{5,4},{6,7},{7,6},{8,9},{9,8},{10,11... | collective-permute-start | bytes 1769480 | tf_op jit(solution)/shard_map/ppermute | solution.py:466
  234.3 41.3 %collective-permute-start.1 = (bf16[2,192,256]{2,1,0:T(8,128)(2,1)}, bf16[2,192,256]{2,1,0:T(8,128)(2,1)}, u32[]{:S(2)}, u32[]{:S(2)}) collective-permute-start(bf16[2,192,256]{2,1,0:T(8,128)(2,1)} %get-tuple-element.60.refs_0_), channel_id=1, source_target_pairs={{0,1},{1,0},{2,3},{3,2},{4,5},{5,4},{6,7},{7,6},{8,9},{9,8},{10,11... | collective-permute-start | bytes 589832 | tf_op jit(solution)/shard_map/ppermute | solution.py:465
  234.3 1.0 copy-start.2
  235.3 40.3 %collective-permute-start.2 = (bf16[2,192,256]{2,1,0:T(8,128)(2,1)S(1)}, bf16[2,192,256]{2,1,0:T(8,128)(2,1)}, u32[]{:S(2)}, u32[]{:S(2)}) collective-permute-start(bf16[2,192,256]{2,1,0:T(8,128)(2,1)S(1)} %collective-permute-done.refs_1_), channel_id=1, source_target_pairs={{0,1},{1,0},{2,3},{3,2},{4,5},{5,4},{6,7},{7,6},{8,9},{9,8},{10,11... | collective-permute-start | bytes 589832 | tf_op jit(solution)/shard_map/ppermute | solution.py:466
  257.3 1.0 copy-start.5
  258.2 1.0 copy-start.6
  259.2 1.0 copy-start.8
  260.2 1.0 copy-start.10
  261.2 1.7 copy-start.1
  262.9 1.2 copy-start.3
  264.1 2.9 %copy-start = (bf16[10,192,256]{2,1,0:T(8,128)(2,1)S(1)}, bf16[10,192,256]{2,1,0:T(8,128)(2,1)}, u32[]{:S(2)}) copy-start(bf16[10,192,256]{2,1,0:T(8,128)(2,1)} %get-tuple-element.62.refs_0_) | copy-start | bytes 2949124
  267.0 4.6 %copy-start.4 = (bf16[6,192,256]{2,1,0:T(8,128)(2,1)S(1)}, bf16[6,192,256]{2,1,0:T(8,128)(2,1)}, u32[]{:S(2)}) copy-start(bf16[6,192,256]{2,1,0:T(8,128)(2,1)} %get-tuple-element.61.refs_0_) | copy-start | bytes 1769476
  271.6 3.9 %copy-start.11 = (bf16[2,192,256]{2,1,0:T(8,128)(2,1)S(1)}, bf16[2,192,256]{2,1,0:T(8,128)(2,1)}, u32[]{:S(2)}) copy-start(bf16[2,192,256]{2,1,0:T(8,128)(2,1)} %get-tuple-element.60.refs_0_) | copy-start | bytes 589828

commit v3 on v2

--- a/solution.py
+++ b/solution.py
@@ -22,12 +22,18 @@
 DEVICES = 16
 ROWS = (64, 16, 64, 64)
 COLS = (192, 256, 256, 256)
+KINDS = 4
+LANES = 128
+WIDE = 256
+THIRD = 48
 PACKED = 192
+PHASES = 4
 SLOTS = 3
 AHEAD = 6
 GROUP = 8
-CHUNKS = (4, 10, 10, 6, 2)
+CHUNKS = (6, 10, 10, 4, 2)
 HEAD = CHUNKS[0]
+LATE = 1
 UPDATE_FLOPS = 2_000_000_000
 ASSEMBLE_FLOPS = 40_000_000
 FIRST_SCALE = 1.0 / (1.0 - BETA_ONE**STEP_COUNT)
@@ -47,44 +53,51 @@
     return P(None, None, "model") if col_split else P(None, "model", None)
 
 
+def split(refs, *sizes):
+    groups, start = [], 0
+    for size in sizes:
+        groups.append(refs[start] if size is None else refs[start : start + size])
+        start += 1 if size is None else size
+    return groups
+
+
 def pack_rest(dst, proj, fcin, fcout):
-    dst[0:64, :] = fcin.astype(jnp.bfloat16)
-    dst[64:128, :] = fcout.astype(jnp.bfloat16)
-    dst[128:144, :] = proj.astype(jnp.bfloat16)
+    start = 0
+    for rows in (fcin, fcout, proj):
+        dst[start : start + rows.shape[0], :] = rows.astype(jnp.bfloat16)
+        start += rows.shape[0]
 
 
 def pack_grad(dst, qkv):
-    wide = qkv[:, 0:128].astype(jnp.bfloat16)
-    thin = qkv[:, 128:192]
-    dst[144:176, 0:128] = wide[0:32]
-    dst[144:176, 128:256] = wide[32:64]
-    left = jnp.concatenate([thin[0:16], thin[16:32]], axis=1)
-    right = jnp.concatenate([thin[32:48], thin[48:64]], axis=1)
-    dst[176:192, 0:128] = left.astype(jnp.bfloat16)
-    dst[176:192, 128:256] = right.astype(jnp.bfloat16)
+    for half in range(2):
+        side = slice(half * LANES, half * LANES + LANES)
+        first = half * 32
+        dst[144:176, side] = qkv[first : first + 32, :LANES].astype(jnp.bfloat16)
+        thin = qkv[first : first + 32, LANES:]
+        dst[176:192, side] = jnp.concatenate([thin[:16], thin[16:]], axis=1).astype(jnp.bfloat16)
 
 
 def pack_turned(dst, qkv):
     turned = jnp.transpose(qkv)
-    left = jnp.concatenate([turned[0:48], turned[96:144]], axis=1)
-    right = jnp.concatenate([turned[48:96], turned[144:192]], axis=1)
-    dst[144:192, 0:128] = left.astype(jnp.bfloat16)
-    dst[144:192, 128:256] = right.astype(jnp.bfloat16)
+    blocks = [turned[THIRD * q : THIRD * (q + 1)] for q in range(4)]
+    for half in range(2):
+        side = slice(half * LANES, half * LANES + LANES)
+        dst[144:192, side] = jnp.concatenate([blocks[half], blocks[half + 2]], axis=1).astype(jnp.bfloat16)
 
 
 def column_sums(scr):
-    folded = scr[:, 0:128] + scr[:, 128:256]
+    folded = scr[:, :LANES] + scr[:, LANES:]
     return jnp.sum(jnp.transpose(folded), axis=0, keepdims=True)
 
 
 def step_kernel(*refs):
-    grads, weights, firsts, seconds = refs[0:4], refs[4:8], refs[8:12], refs[12:16]
-    out_g, out_coef, out_ratio, out_far = refs[16:20], refs[20], refs[21], refs[22]
-    out_b = refs[23 : 23 + len(CHUNKS)]
-    scr = refs[23 + len(CHUNKS) :]
-    stage, w_buf, m_buf, v_buf, g_buf = scr[0:4], scr[4:8], scr[8:12], scr[12:16], scr[16:20]
-    turned, snd, rcv, n_acc, wn_acc, un_acc, coef, ratio, sync_src, sync_buf = scr[20:30]
-    load_sem, state_sem, send_sem, recv_sem, sync_send, sync_recv, far_sem, out_sem, grad_sem = scr[30:39]
+    operands, out_g, (out_coef, out_ratio, out_far), out_b, buffers, singles, sems = split(
+        refs, KINDS * 4, KINDS, 3, len(CHUNKS), KINDS * 5, 10, 9
+    )
+    grads, weights, firsts, seconds = split(operands, *[KINDS] * 4)
+    stage, w_buf, m_buf, v_buf, g_buf = split(buffers, *[KINDS] * 5)
+    turned, snd, rcv, n_acc, wn_acc, un_acc, coef, ratio, sync_src, sync_buf = singles
+    load_sem, state_sem, send_sem, recv_sem, sync_send, sync_recv, far_sem, out_sem, grad_sem = sems
 
     d = lax.axis_index("data")
     m = lax.axis_index("model")
@@ -94,7 +107,7 @@
         return (dev // DATA, dev % DATA)
 
     def loads(layer, slot):
-        return [pltpu.make_async_copy(grads[a].at[0, layer], stage[a].at[slot], load_sem.at[slot, a]) for a in range(4)]
+        return [pltpu.make_async_copy(grads[a].at[0, layer], stage[a].at[slot], load_sem.at[slot, a]) for a in range(KINDS)]
 
     for layer in range(SLOTS):
         for copy in loads(layer, layer):
@@ -151,7 +164,7 @@
 
     state_copies = []
     for idx, (source, target) in enumerate(((weights, w_buf), (firsts, m_buf), (seconds, v_buf))):
-        for a in range(4):
+        for a in range(KINDS):
             copy = pltpu.make_async_copy(source[a], target[a], state_sem.at[idx, a])
             copy.start()
             state_copies.append(copy)
@@ -170,7 +183,7 @@
         def _():
             produce(layer + AHEAD)
 
-        for a in range(4):
+        for a in range(KINDS):
             w = w_buf[a][layer]
             wn_acc[pl.ds(a * LAYERS + layer, 1), 0 : COLS[a]] = jnp.sum(w * w, axis=0, keepdims=True)
             m_buf[a][layer] = (BETA_ONE * FIRST_SCALE) * m_buf[a][layer]
@@ -193,23 +206,21 @@
         proj = gathered(128, 16)
         g_buf[1][layer] = proj
         wide = gathered(144, 32)
-        g_buf[0][layer, 0:32, 0:128] = wide[:, 0:128]
-        g_buf[0][layer, 32:64, 0:128] = wide[:, 128:256]
+        for half in range(2):
+            g_buf[0][layer, 32 * half : 32 * half + 32, :LANES] = wide[:, LANES * half : LANES * half + LANES]
         thin = gathered(176, 16)
         for q in range(4):
-            g_buf[0][layer, 16 * q : 16 * q + 16, 128:192] = thin[:, 64 * q : 64 * q + 64]
+            g_buf[0][layer, 16 * q : 16 * q + 16, LANES:] = thin[:, 64 * q : 64 * q + 64]
         n_acc[...] += squares(fcin) + squares(fcout) + squares(proj) + squares(wide) + squares(thin)
 
         @pl.when(lax.rem(layer, GROUP) == GROUP - 1)
         def _():
-            for a in range(4):
+            for a in range(KINDS):
                 grad_copy(a, layer // GROUP).start()
 
         return carry
 
     lax.fori_loop(0, LAYERS, consume, 0)
-
-    row_idx = lax.broadcasted_iota(jnp.int32, (8, 128), 0)
 
     def tile_copy(phase, slot, dev):
         return pltpu.make_async_remote_copy(
@@ -240,17 +251,16 @@
         lax.fori_loop(1, DEVICES, receive, 0)
         return jnp.sum(sync_buf[phase], axis=0)
 
-    n_row = jnp.sum(n_acc[:, 0:128] + n_acc[:, 128:256], axis=0, keepdims=True)
-    share(0, jnp.where(row_idx == 0, n_row, 0.0))
-    share(1, jnp.where(row_idx == 0, column_sums(wn_acc), 0.0))
-    total_norm = jnp.sqrt(jnp.sum(collect(0)[0:1, :], axis=1, keepdims=True))
+    share(0, jnp.sum(n_acc[:, :LANES] + n_acc[:, LANES:], axis=0, keepdims=True))
+    share(1, column_sums(wn_acc))
+    total_norm = jnp.sqrt(jnp.sum(collect(0), axis=1, keepdims=True))
     clip_coef = jnp.minimum(1.0, MAX_NORM / total_norm)
-    coef[...] = jnp.broadcast_to(clip_coef, (8, 128))
+    coef[...] = jnp.broadcast_to(clip_coef, coef.shape)
     first_coef = ((1.0 - BETA_ONE) * FIRST_SCALE) * clip_coef
     second_coef = ((1.0 - BETA_TWO) * SECOND_SCALE) * clip_coef * clip_coef
 
     def direction(layer, carry):
-        for a in range(4):
+        for a in range(KINDS):
             g = g_buf[a][layer]
             first_hat = m_buf[a][layer] + first_coef * g
             second_hat = v_buf[a][layer] + second_coef * (g * g)
@@ -261,13 +271,13 @@
 
     def set_ratio(weight_sq, update_sq):
         scaled = LEARN_RATE * (jnp.sqrt(weight_sq) / jnp.sqrt(update_sq))
-        spread = jnp.transpose(jnp.broadcast_to(scaled, (128, 128)))
-        ratio[:, 0:128] = spread
-        ratio[:, 128:256] = spread
+        spread = jnp.transpose(jnp.broadcast_to(scaled, (LANES, LANES)))
+        ratio[:, :LANES] = spread
+        ratio[:, LANES:] = spread
 
     def finish(layer, carry):
         rows = []
-        for a in range(4):
+        for a in range(KINDS):
             factor = ratio[pl.ds(a * LAYERS + layer, 1), 0 : COLS[a]]
             rows.append(w_buf[a][layer] - factor * m_buf[a][layer])
         pack_rest(snd.at[0, layer], *rows[1:])
@@ -284,37 +294,60 @@
     def replica_copy(i):
         return pltpu.make_async_copy(snd.at[0, pl.ds(starts[i], CHUNKS[i])], out_b[i], out_sem.at[i])
 
-    far = pltpu.make_async_remote_copy(
-        src_ref=snd.at[0, pl.ds(0, HEAD)],
-        dst_ref=out_far,
-        send_sem=far_sem.at[0],
-        recv_sem=far_sem.at[1],
-        device_id=(m, (d + 2) % DATA),
-        device_id_type=MESH,
-    )
+    def far(layer):
+        return pltpu.make_async_remote_copy(
+            src_ref=snd.at[0, layer],
+            dst_ref=out_far.at[layer],
+            send_sem=far_sem.at[0, layer],
+            recv_sem=far_sem.at[1, layer],
+            device_id=(m, (d + 2) % DATA),
+            device_id_type=MESH,
+        )
+
+    def finish_and_send(layer, carry):
+        finish(layer, carry)
+
+        @pl.when(d % 2 == 1)
+        def _():
+            far(layer).start()
+
+        return carry
+
+    def send_late(layer, carry):
+        @pl.when(d % 2 == 0)
+        def _():
+            far(layer).start()
+
+        return carry
+
+    def far_done(layer, carry):
+        far(layer).wait()
+        return carry
+
     coef_copy = pltpu.make_async_copy(coef, out_coef, out_sem.at[len(CHUNKS)])
     ratio_copy = pltpu.make_async_copy(ratio, out_ratio, out_sem.at[len(CHUNKS) + 1])
 
-    lane = lax.broadcasted_iota(jnp.int32, (1, 128), 1) % LAYERS
+    lane = lax.broadcasted_iota(jnp.int32, (1, LANES), 1) % LAYERS
     lax.fori_loop(0, HEAD, direction, 0)
-    share(2, jnp.where(row_idx == 0, column_sums(un_acc), 0.0))
+    share(2, column_sums(un_acc))
     coef_copy.start()
     lax.fori_loop(0, LAYERS, sent, 0)
     lax.fori_loop(HEAD, LAYERS, direction, 0)
-    share(3, jnp.where(row_idx == 0, column_sums(un_acc), 0.0))
-    weight_sq = collect(1)[0:1, :]
-    set_ratio(weight_sq, jnp.where(lane < HEAD, collect(2)[0:1, :], 1.0))
-    lax.fori_loop(0, HEAD, finish, 0)
-    far.start()
+    share(3, column_sums(un_acc))
+    weight_sq = collect(1)
+    set_ratio(weight_sq, jnp.where(lane < HEAD, collect(2), 1.0))
+    lax.fori_loop(0, HEAD, finish_and_send, 0)
     replica_copy(0).start()
-    set_ratio(weight_sq, collect(3)[0:1, :])
+    set_ratio(weight_sq, collect(3))
     ratio_copy.start()
     for i in range(1, len(CHUNKS)):
         lax.fori_loop(starts[i], starts[i] + CHUNKS[i], finish, 0)
         replica_copy(i).start()
+        if i == LATE:
+            lax.fori_loop(0, HEAD, send_late, 0)
 
     def drain(off, carry):
-        for phase in range(4):
+        for phase in range(PHASES):
             tile_copy(phase, gid, (gid + off) % DEVICES).wait_send()
         return carry
 
@@ -322,64 +355,51 @@
     coef_copy.wait()
     ratio_copy.wait()
     for group in range(LAYERS // GROUP):
-        for a in range(4):
+        for a in range(KINDS):
             grad_copy(a, group).wait()
     for i in range(len(CHUNKS)):
         replica_copy(i).wait()
-    far.wait()
+    lax.fori_loop(0, HEAD, far_done, 0)
 
 
 def run_step(grads, weights, firsts, seconds):
     state_shapes = [jax.ShapeDtypeStruct(w.shape, jnp.float32) for w in weights]
     pieces = [jax.ShapeDtypeStruct((n, PACKED, 256), jnp.bfloat16) for n in CHUNKS]
-    small = [jax.ShapeDtypeStruct((8, 128), jnp.float32), jax.ShapeDtypeStruct((128, 256), jnp.float32)]
-    state_scratch = [pltpu.VMEM((LAYERS, ROWS[a], COLS[a]), jnp.float32) for a in range(4)]
-    scratch = [pltpu.VMEM((SLOTS, g.shape[2], g.shape[3]), jnp.float32) for g in grads]
-    scratch += state_scratch * 4
-    scratch += [
-        pltpu.VMEM((256, 192), jnp.float32),
-        pltpu.VMEM((3, LAYERS, PACKED, 256), jnp.bfloat16),
-        pltpu.VMEM((4, LAYERS, PACKED, 256), jnp.bfloat16),
-        pltpu.VMEM((8, 256), jnp.float32),
-        pltpu.VMEM((128, 256), jnp.float32),
-        pltpu.VMEM((128, 256), jnp.float32),
-        pltpu.VMEM((8, 128), jnp.float32),
-        pltpu.VMEM((128, 256), jnp.float32),
-        pltpu.VMEM((4, 8, 128), jnp.float32),
-        pltpu.VMEM((4, DEVICES, 8, 128), jnp.float32),
-        pltpu.SemaphoreType.DMA((SLOTS, 4)),
-        pltpu.SemaphoreType.DMA((3, 4)),
-        pltpu.SemaphoreType.DMA((3, LAYERS)),
-        pltpu.SemaphoreType.DMA((3, LAYERS)),
-        pltpu.SemaphoreType.DMA((4, DEVICES)),
-        pltpu.SemaphoreType.DMA((4, DEVICES)),
-        pltpu.SemaphoreType.DMA((2,)),
-        pltpu.SemaphoreType.DMA((len(CHUNKS) + 2,)),
-        pltpu.SemaphoreType.DMA((4, LAYERS // GROUP)),
-    ]
+    row = (1, LANES)
+    table = (LANES, WIDE)
+    small = [jax.ShapeDtypeStruct(shape, jnp.float32) for shape in (row, table)]
+    scratch = [pltpu.VMEM((SLOTS, *g.shape[2:]), jnp.float32) for g in grads]
+    scratch += [pltpu.VMEM((LAYERS, ROWS[a], COLS[a]), jnp.float32) for a in range(KINDS)] * 4
+    scratch += [pltpu.VMEM((WIDE, COLS[0]), jnp.float32)]
+    scratch += [pltpu.VMEM((n, LAYERS, PACKED, WIDE), jnp.bfloat16) for n in (DATA - 1, DATA)]
+    shapes = [(8, WIDE), table, table, row, table, (PHASES, *row), (PHASES, DEVICES, *row)]
+    scratch += [pltpu.VMEM(shape, jnp.float32) for shape in shapes]
+    exchange_shape = (DATA - 1, LAYERS)
+    sync_shape = (PHASES, DEVICES)
+    shapes = [(SLOTS, KINDS), (3, KINDS), exchange_shape, exchange_shape, sync_shape, sync_shape]
+    shapes += [(2, HEAD), (len(CHUNKS) + 2,), (KINDS, LAYERS // GROUP)]
+    scratch += [pltpu.SemaphoreType.DMA(shape) for shape in shapes]
     anywhere = pl.BlockSpec(memory_space=pl.ANY)
-    out_shape = state_shapes + small + pieces[:1] + pieces
+    out_shape = state_shapes + small + [pieces[0]] + pieces
     results = pl.pallas_call(
         step_kernel,
         out_shape=out_shape,
-        in_specs=[anywhere] * 16,
+        in_specs=[anywhere] * (KINDS * 4),
         out_specs=[anywhere] * len(out_shape),
         scratch_shapes=scratch,
         compiler_params=pltpu.CompilerParams(collective_id=0, has_side_effects=True, vmem_limit_bytes=63 << 20),
         name="lamb_step",
     )(*grads, *weights, *firsts, *seconds)
-    return results[0:4], results[4], results[5], results[6], results[7:]
+    return split(results, KINDS, None, None, None, len(CHUNKS))
 
 
 def update_kernel(*refs):
-    coef, ratio = refs[0], refs[1]
-    means, weights, firsts, seconds = refs[2:6], refs[6:10], refs[10:14], refs[14:18]
-    out_w, out_m, out_v = refs[18:22], refs[22:26], refs[26:30]
-    clip_coef = coef[0:1, 0:1]
+    coef, ratio, means, weights, firsts, seconds, out_w, out_m, out_v = split(refs, None, None, *[KINDS] * 7)
+    clip_coef = coef[:, :1]
     block = means[0].shape[0]
     for b in range(block):
         layer = pl.program_id(0) * block + b
-        for a in range(4):
+        for a in range(KINDS):
             w = weights[a][b]
             clipped = clip_coef * means[a][b]
             first = BETA_ONE * firsts[a][b] + (1.0 - BETA_ONE) * clipped
@@ -392,12 +412,12 @@
 
 def update(coef, ratio, means, weights, firsts, seconds):
     block = 2
-    layer_specs = [pl.BlockSpec((block, ROWS[a], COLS[a]), lambda i: (i, 0, 0)) for a in range(4)]
+    layer_specs = [pl.BlockSpec((block, ROWS[a], COLS[a]), lambda i: (i, 0, 0)) for a in range(KINDS)]
     return pl.pallas_call(
         update_kernel,
         grid=(LAYERS // block,),
         out_shape=[jax.ShapeDtypeStruct(w.shape, jnp.float32) for w in weights] * 3,
-        in_specs=[pl.BlockSpec((8, 128), lambda i: (0, 0)), pl.BlockSpec((128, 256), lambda i: (0, 0))] + layer_specs * 4,
+        in_specs=[pl.BlockSpec(table.shape, lambda i: (0, 0)) for table in (coef, ratio)] + layer_specs * 4,
         out_specs=layer_specs * 3,
         cost_estimate=pl.CostEstimate(flops=UPDATE_FLOPS, bytes_accessed=47_000_000, transcendentals=0),
         compiler_params=pltpu.CompilerParams(vmem_limit_bytes=60 << 20),
@@ -406,8 +426,7 @@
 
 
 def assemble_kernel(has_alias, *refs):
-    shards = refs[0:4]
-    qkv, proj, fcin, fcout, parts = refs[4 + 4 * has_alias :]
+    shards, _, (qkv, proj, fcin, fcout), parts = split(refs, DATA, KINDS * has_alias, KINDS, None)
     d = lax.axis_index("data")
     partner = d + 1 - 2 * (d % 2)
     owners = (d, (d + 2) % DATA, partner, (partner + 2) % DATA)
@@ -419,10 +438,12 @@
         proj[:, small, :] = shard[:, 128:144, :]
         parts[owner] = shard[:, 144:192, :]
     for half in range(2):
+        side = slice(half * LANES, half * LANES + LANES)
         first, second = parts[2 * half], parts[2 * half + 1]
-        for q, lane in ((0, 0), (48, 128), (96, 64), (144, 192)):
-            pair = jnp.concatenate([first[:, :, lane : lane + 64], second[:, :, lane : lane + 64]], axis=2)
-            qkv[:, q : q + 48, 128 * half : 128 * half + 128] = pair
+        for q in range(4):
+            lane = (q % 2) * LANES + (q // 2) * 64
+            pair = jnp.concatenate([shard[:, :, lane : lane + 64] for shard in (first, second)], axis=2)
+            qkv[:, THIRD * q : THIRD * (q + 1), side] = pair
 
 
 def assemble(chunk, shards, previous):

time: 279 us -> 274 us (0.982)
  waiting for transfers between devices: 60 us -> 53.8 us
  Pallas kernels: 202 us -> 205 us
    ppermute x4, waiting for transfers between devices: 60 us -> 47.8 us  [device_step(): far = lax.ppermute(own, 'data', across) if chunk else far_head]
    ppermute x5, waiting for transfers between devices: 0.01 us -> 5.96 us  [device_step(): far_near = lax.ppermute(far, 'data', on_chip)]
    pallas_call x1, Pallas kernels: 166 us -> 169 us  [run_step(): pl.pallas_call(step_kernel, out_shape=out_shape, in_specs=[anywhere] * (K...]
where the time goes in v3:
time: 274 us; the launch traced here: 273 us
  Pallas kernels  205 us (75%)
  waiting for transfers between devices  53.8 us (20%)
  local copies, waits for them, and re-layouts  7.13 us (3%)
  starting transfers between devices  6.17 us (2%)
    pallas_call x1, Pallas kernels, run_step(): pl.pallas_call(step_kernel, out_shape=out_shape, in_specs=[anywhere] * (K...  169 us
    ppermute x4, waiting for transfers between devices, device_step(): far = lax.ppermute(own, 'data', across) if chunk else far_head  47.8 us
    pallas_call x1, Pallas kernels, update(): pl.pallas_call(update_kernel, grid=(LAYERS // block,), out_shape=[jax.Sha...  22.2 us
    pallas_call x5, Pallas kernels, assemble(): pl.pallas_call(functools.partial(assemble_kernel, bool(previous)), grid=(...  13.8 us
    unnamed x24, local copies, waits for them, and re-layouts  7.13 us
    ppermute x5, waiting for transfers between devices, device_step(): far_near = lax.ppermute(far, 'data', on_chip)  5.96 us
  transfers between devices with their start and end apart: 14, of which 2 were waited for; matrix products, arithmetic and copies ran while one was open for 0% of the time, Pallas kernels for 12%

profile of v3, /device:TPU:0, one launch (start us, length us, event | category | flops | bytes accessed | tf_op | source)
XLA Modules:
  0.0 273.2 jit_solution(11231530369534800532)
XLA Ops:
  0.6 169.3 %lamb_step.1 = (f32[32,64,192]{2,1,0:T(8,128)}, f32[32,16,256]{2,1,0:T(8,128)}, f32[32,64,256]{2,1,0:T(8,128)}, f32[32,64,256]{2,1,0:T(8,128)}, f32[1,128]{1,0:T...) custom-call(f32[1,32,192,256]{3,2,1,0:T(8,128)} %bitcast.3, ...), custom_call_target="tpu_custom_call" | custom-call | tf_op jit(solution)/shard_map/lamb_step/pallas_call | solution.py:384
  169.9 1.1 collective-permute-start.9
  171.1 0.9 collective-permute-start.6
  172.0 1.1 collective-permute-start.3
  173.1 0.0 collective-permute-start.12
  173.1 0.9 collective-permute-start
  174.0 47.8 %collective-permute-done.refs_1_ = bf16[2,192,256]{2,1,0:T(8,128)(2,1)S(1)} collective-permute-done((bf16[2,192,256]{2,1,0:T(8,128)(2,1)}, bf16[2,192,256]{2,1,0:T(8,128)(2,1)S(1)}, u32[]{:S(2)}, u32[]{:S(2)}) %collective-permute-start) | collective-permute-done | bytes 196640 | tf_op jit(solution)/shard_map/ppermute | solution.py:485
  221.8 0.0 collective-permute-start.10
  221.8 0.0 collective-permute-done.3.refs_1_
  221.8 0.5 collective-permute-start.7
  222.4 0.0 collective-permute-done.9.refs_1_
  222.4 0.0 collective-permute-start.11
  222.4 0.0 collective-permute-done.6.refs_1_
  222.4 0.5 collective-permute-start.8
  222.9 0.0 collective-permute-done.12.refs_2_
  222.9 0.0 copy-start.6
  222.9 0.8 copy-done.6
  223.7 0.0 collective-permute-start.13
  223.7 5.9 %collective-permute-done.13.refs_3_ = bf16[6,192,256]{2,1,0:T(8,128)(2,1)S(1)} collective-permute-done((bf16[6,192,256]{2,1,0:T(8,128)(2,1)}, bf16[6,192,256]{2,1,0:T(8,128)(2,1)S(1)}, u32[]{:S(2)}, u32[]{:S(2)}) %collective-permute-start.13) | collective-permute-done | bytes 589856 | tf_op jit(solution)/shard_map/ppermute | solution.py:487
  229.7 0.0 copy-start.8
  229.7 0.8 copy-done.8
  230.5 0.1 collective-permute-start.4
  230.6 0.0 collective-permute-done.10.refs_2_
  230.6 0.4 collective-permute-start.5
  231.0 0.0 collective-permute-done.7.refs_2_
  231.0 0.1 collective-permute-start.1
  231.2 0.0 collective-permute-done.11.refs_3_
  231.2 0.0 copy-start.2
  231.2 1.0 copy-done.2
  232.1 0.4 collective-permute-start.2
  232.5 22.2 %update.1 = (f32[32,64,192]{2,1,0:T(8,128)}, f32[32,16,256]{2,1,0:T(8,128)}, f32[32,64,256]{2,1,0:T(8,128)}, f32[32,64,256]{2,1,0:T(8,128)}, f32[32,64,192]{2,1,...) custom-call(f32[1,128]{1,0:T(1,128)} %get-tuple-element.86.refs_0_, ...), custom_call_target="tpu_custom_call" | custom-call | flops 2000000000 | bytes 47000000 | tf_op jit(solution)/shard_map/update/pallas_call | solution.py:416
  254.7 0.0 copy-start.4
  254.7 1.1 copy-done.4
  255.8 0.0 copy-start.5
  255.8 1.1 copy-done.5
  256.9 0.0 copy-start.7
  256.9 1.1 copy-done.7
  257.9 0.0 copy-start.9
  257.9 1.1 copy-done.9
  259.0 0.0 copy-start.1
  259.0 0.0 copy-start.3
  259.0 1.9 assemble.5
  260.9 0.0 copy-done.1
  260.9 0.3 copy-done.3
  261.2 0.0 copy-start
  261.2 2.9 %assemble.6 = (bf16[32,192,256]{2,1,0:T(8,128)(2,1)}, bf16[32,64,256]{2,1,0:T(8,128)(2,1)}, bf16[32,256,256]{2,1,0:T(8,128)(2,1)}, bf16[32,256,256]{2,1,0:T(8,128)(2,1)}) custom-call(bf16[10,192,256]{2,1,0:T(8,128)(2,1)S(1)} %copy-done.1, ...), custom_call_target="tpu_custom_call", output_to_operand_aliasing={{0}: (4, {}), {1}: (5, {}), {2}: (6, {}), {3}: (7, {})} | custom-call | flops 400000000 | bytes 8000000 | tf_op jit(solution)/shard_map/assemble/pallas_call | solution.py:455
  264.1 0.0 collective-permute-done.8.refs_3_
  264.1 0.0 copy-done
  264.1 0.0 copy-start.10
  264.1 4.6 %assemble.7 = (bf16[32,192,256]{2,1,0:T(8,128)(2,1)}, bf16[32,64,256]{2,1,0:T(8,128)(2,1)}, bf16[32,256,256]{2,1,0:T(8,128)(2,1)}, bf16[32,256,256]{2,1,0:T(8,128)(2,1)}) custom-call(bf16[10,192,256]{2,1,0:T(8,128)(2,1)S(1)} %copy-done, ...), custom_call_target="tpu_custom_call", output_to_operand_aliasing={{0}: (4, {}), {1}: (5, {}), {2}: (6, {}), {3}: (7, {})} | custom-call | flops 400000000 | bytes 8000000 | tf_op jit(solution)/shard_map/assemble/pallas_call | solution.py:455
  268.7 0.0 collective-permute-done.4.refs_2_
  268.7 0.0 collective-permute-done.5.refs_3_
  268.7 0.0 copy-done.10
  268.8 0.0 copy-start.11
  268.8 2.4 assemble.8
  271.2 0.0 collective-permute-done.1.refs_2_
  271.2 0.0 collective-permute-done.2.refs_3_
  271.2 0.0 copy-done.11
  271.2 2.0 assemble.9
Async XLA Ops:
  169.9 52.4 %collective-permute-start.9 = (bf16[10,192,256]{2,1,0:T(8,128)(2,1)}, bf16[10,192,256]{2,1,0:T(8,128)(2,1)S(1)}, u32[]{:S(2)}, u32[]{:S(2)}) collective-permute-start(bf16[10,192,256]{2,1,0:T(8,128)(2,1)} %get-tuple-element.63.refs_0_), channel_id=1, source_target_pairs={{0,2},{1,3},{2,0},{3,1},{4,6},{5,7},{6,4},{7,5},{8,10},{9,11},{10,... | collective-permute-start | bytes 2949128 | tf_op jit(solution)/shard_map/ppermute | solution.py:485
  171.1 51.3 %collective-permute-start.6 = (bf16[10,192,256]{2,1,0:T(8,128)(2,1)}, bf16[10,192,256]{2,1,0:T(8,128)(2,1)S(1)}, u32[]{:S(2)}, u32[]{:S(2)}) collective-permute-start(bf16[10,192,256]{2,1,0:T(8,128)(2,1)} %get-tuple-element.62.refs_0_), channel_id=1, source_target_pairs={{0,2},{1,3},{2,0},{3,1},{4,6},{5,7},{6,4},{7,5},{8,10},{9,11},{10,... | collective-permute-start | bytes 2949128 | tf_op jit(solution)/shard_map/ppermute | solution.py:485
  172.0 49.8 %collective-permute-start.3 = (bf16[4,192,256]{2,1,0:T(8,128)(2,1)}, bf16[4,192,256]{2,1,0:T(8,128)(2,1)}, u32[]{:S(2)}, u32[]{:S(2)}) collective-permute-start(bf16[4,192,256]{2,1,0:T(8,128)(2,1)} %get-tuple-element.61.refs_0_), channel_id=1, source_target_pairs={{0,2},{1,3},{2,0},{3,1},{4,6},{5,7},{6,4},{7,5},{8,10},{9,11},{10,... | collective-permute-start | bytes 1179656 | tf_op jit(solution)/shard_map/ppermute | solution.py:485
  173.1 49.8 %collective-permute-start.12 = (bf16[6,192,256]{2,1,0:T(8,128)(2,1)}, bf16[6,192,256]{2,1,0:T(8,128)(2,1)S(1)}, u32[]{:S(2)}, u32[]{:S(2)}) collective-permute-start(bf16[6,192,256]{2,1,0:T(8,128)(2,1)} %get-tuple-element.64.refs_0_), channel_id=1, source_target_pairs={{0,1},{1,0},{2,3},{3,2},{4,5},{5,4},{6,7},{7,6},{8,9},{9,8},{10,11... | collective-permute-start | bytes 1769480 | tf_op jit(solution)/shard_map/ppermute | solution.py:486
  173.1 48.7 %collective-permute-start = (bf16[2,192,256]{2,1,0:T(8,128)(2,1)}, bf16[2,192,256]{2,1,0:T(8,128)(2,1)S(1)}, u32[]{:S(2)}, u32[]{:S(2)}) collective-permute-start(bf16[2,192,256]{2,1,0:T(8,128)(2,1)} %get-tuple-element.60.refs_0_), channel_id=1, source_target_pairs={{0,2},{1,3},{2,0},{3,1},{4,6},{5,7},{6,4},{7,5},{8,10},{9,11},{10,... | collective-permute-start | bytes 589832 | tf_op jit(solution)/shard_map/ppermute | solution.py:485
  221.8 8.8 %collective-permute-start.10 = (bf16[10,192,256]{2,1,0:T(8,128)(2,1)}, bf16[10,192,256]{2,1,0:T(8,128)(2,1)S(1)}, u32[]{:S(2)}, u32[]{:S(2)}) collective-permute-start(bf16[10,192,256]{2,1,0:T(8,128)(2,1)} %get-tuple-element.63.refs_0_), channel_id=1, source_target_pairs={{0,1},{1,0},{2,3},{3,2},{4,5},{5,4},{6,7},{7,6},{8,9},{9,8},{10,11... | collective-permute-start | bytes 2949128 | tf_op jit(solution)/shard_map/ppermute | solution.py:486
  221.8 9.2 %collective-permute-start.7 = (bf16[10,192,256]{2,1,0:T(8,128)(2,1)}, bf16[10,192,256]{2,1,0:T(8,128)(2,1)S(1)}, u32[]{:S(2)}, u32[]{:S(2)}) collective-permute-start(bf16[10,192,256]{2,1,0:T(8,128)(2,1)} %get-tuple-element.62.refs_0_), channel_id=1, source_target_pairs={{0,1},{1,0},{2,3},{3,2},{4,5},{5,4},{6,7},{7,6},{8,9},{9,8},{10,11... | collective-permute-start | bytes 2949128 | tf_op jit(solution)/shard_map/ppermute | solution.py:486
  222.4 8.8 %collective-permute-start.11 = (bf16[10,192,256]{2,1,0:T(8,128)(2,1)S(1)}, bf16[10,192,256]{2,1,0:T(8,128)(2,1)S(1)}, u32[]{:S(2)}, u32[]{:S(2)}) collective-permute-start(bf16[10,192,256]{2,1,0:T(8,128)(2,1)S(1)} %collective-permute-done.9.refs_1_), channel_id=1, source_target_pairs={{0,1},{1,0},{2,3},{3,2},{4,5},{5,4},{6,7},{7,6},{8,9},{9,8},{10,11... | collective-permute-start | bytes 2949128 | tf_op jit(solution)/shard_map/ppermute | solution.py:487
  222.4 41.7 %collective-permute-start.8 = (bf16[10,192,256]{2,1,0:T(8,128)(2,1)S(1)}, bf16[10,192,256]{2,1,0:T(8,128)(2,1)}, u32[]{:S(2)}, u32[]{:S(2)}) collective-permute-start(bf16[10,192,256]{2,1,0:T(8,128)(2,1)S(1)} %collective-permute-done.6.refs_1_), channel_id=1, source_target_pairs={{0,1},{1,0},{2,3},{3,2},{4,5},{5,4},{6,7},{7,6},{8,9},{9,8},{10,11... | collective-permute-start | bytes 2949128 | tf_op jit(solution)/shard_map/ppermute | solution.py:487
  222.9 0.8 copy-start.6
  223.7 6.0 %collective-permute-start.13 = (bf16[6,192,256]{2,1,0:T(8,128)(2,1)}, bf16[6,192,256]{2,1,0:T(8,128)(2,1)S(1)}, u32[]{:S(2)}, u32[]{:S(2)}) collective-permute-start(bf16[6,192,256]{2,1,0:T(8,128)(2,1)} %get-tuple-element.65.refs_1_), channel_id=1, source_target_pairs={{0,1},{1,0},{2,3},{3,2},{4,5},{5,4},{6,7},{7,6},{8,9},{9,8},{10,11... | collective-permute-start | bytes 1769480 | tf_op jit(solution)/shard_map/ppermute | solution.py:487
  229.7 0.8 copy-start.8
  230.5 38.2 %collective-permute-start.4 = (bf16[4,192,256]{2,1,0:T(8,128)(2,1)}, bf16[4,192,256]{2,1,0:T(8,128)(2,1)}, u32[]{:S(2)}, u32[]{:S(2)}) collective-permute-start(bf16[4,192,256]{2,1,0:T(8,128)(2,1)} %get-tuple-element.61.refs_0_), channel_id=1, source_target_pairs={{0,1},{1,0},{2,3},{3,2},{4,5},{5,4},{6,7},{7,6},{8,9},{9,8},{10,11... | collective-permute-start | bytes 1179656 | tf_op jit(solution)/shard_map/ppermute | solution.py:486
  230.6 38.1 %collective-permute-start.5 = (bf16[4,192,256]{2,1,0:T(8,128)(2,1)}, bf16[4,192,256]{2,1,0:T(8,128)(2,1)}, u32[]{:S(2)}, u32[]{:S(2)}) collective-permute-start(bf16[4,192,256]{2,1,0:T(8,128)(2,1)} %collective-permute-done.3.refs_1_), channel_id=1, source_target_pairs={{0,1},{1,0},{2,3},{3,2},{4,5},{5,4},{6,7},{7,6},{8,9},{9,8},{10,11... | collective-permute-start | bytes 1179656 | tf_op jit(solution)/shard_map/ppermute | solution.py:487
  231.0 40.1 %collective-permute-start.1 = (bf16[2,192,256]{2,1,0:T(8,128)(2,1)}, bf16[2,192,256]{2,1,0:T(8,128)(2,1)}, u32[]{:S(2)}, u32[]{:S(2)}) collective-permute-start(bf16[2,192,256]{2,1,0:T(8,128)(2,1)} %get-tuple-element.60.refs_0_), channel_id=1, source_target_pairs={{0,1},{1,0},{2,3},{3,2},{4,5},{5,4},{6,7},{7,6},{8,9},{9,8},{10,11... | collective-permute-start | bytes 589832 | tf_op jit(solution)/shard_map/ppermute | solution.py:486
  231.2 1.0 copy-start.2
  232.1 39.1 %collective-permute-start.2 = (bf16[2,192,256]{2,1,0:T(8,128)(2,1)S(1)}, bf16[2,192,256]{2,1,0:T(8,128)(2,1)}, u32[]{:S(2)}, u32[]{:S(2)}) collective-permute-start(bf16[2,192,256]{2,1,0:T(8,128)(2,1)S(1)} %collective-permute-done.refs_1_), channel_id=1, source_target_pairs={{0,1},{1,0},{2,3},{3,2},{4,5},{5,4},{6,7},{7,6},{8,9},{9,8},{10,11... | collective-permute-start | bytes 589832 | tf_op jit(solution)/shard_map/ppermute | solution.py:487
  254.7 1.1 copy-start.4
  255.8 1.1 copy-start.5
  256.9 1.1 copy-start.7
  257.9 1.1 copy-start.9
  259.0 1.9 copy-start.1
  259.0 2.2 copy-start.3
  261.2 2.9 %copy-start = (bf16[10,192,256]{2,1,0:T(8,128)(2,1)S(1)}, bf16[10,192,256]{2,1,0:T(8,128)(2,1)}, u32[]{:S(2)}) copy-start(bf16[10,192,256]{2,1,0:T(8,128)(2,1)} %get-tuple-element.62.refs_0_) | copy-start | bytes 2949124
  264.1 4.6 %copy-start.10 = (bf16[4,192,256]{2,1,0:T(8,128)(2,1)S(1)}, bf16[4,192,256]{2,1,0:T(8,128)(2,1)}, u32[]{:S(2)}) copy-start(bf16[4,192,256]{2,1,0:T(8,128)(2,1)} %get-tuple-element.61.refs_0_) | copy-start | bytes 1179652
  268.8 2.4 copy-start.11

commit v4 on v3

--- a/solution.py
+++ b/solution.py
@@ -33,7 +33,6 @@
 GROUP = 8
 CHUNKS = (6, 10, 10, 4, 2)
 HEAD = CHUNKS[0]
-LATE = 1
 UPDATE_FLOPS = 2_000_000_000
 ASSEMBLE_FLOPS = 40_000_000
 FIRST_SCALE = 1.0 / (1.0 - BETA_ONE**STEP_COUNT)
@@ -101,10 +100,12 @@
 
     d = lax.axis_index("data")
     m = lax.axis_index("model")
-    gid = m * DATA + d
-
-    def coords(dev):
-        return (dev // DATA, dev % DATA)
+
+    def flipped(index, bits):
+        high, low = (index // 2 + bits // 2) % 2, (index + bits) % 2
+        return 2 * high + low
+
+    peers = [(s, (flipped(m, s // DATA), flipped(d, s % DATA))) for s in range(DEVICES - 1, 0, -1)]
 
     def loads(layer, slot):
         return [pltpu.make_async_copy(grads[a].at[0, layer], stage[a].at[slot], load_sem.at[slot, a]) for a in range(KINDS)]
@@ -115,11 +116,8 @@
 
     barrier = pltpu.get_barrier_semaphore()
 
-    def greet(off, carry):
-        pl.semaphore_signal(barrier, inc=1, device_id=coords((gid + off) % DEVICES), device_id_type=MESH)
-        return carry
-
-    lax.fori_loop(1, DEVICES, greet, 0)
+    for _, peer in peers:
+        pl.semaphore_signal(barrier, inc=1, device_id=peer, device_id_type=MESH)
 
     def exchange(layer, k):
         return pltpu.make_async_remote_copy(
@@ -222,33 +220,28 @@
 
     lax.fori_loop(0, LAYERS, consume, 0)
 
-    def tile_copy(phase, slot, dev):
-        return pltpu.make_async_remote_copy(
-            src_ref=sync_src.at[phase],
-            dst_ref=sync_buf.at[phase, slot],
-            send_sem=sync_send.at[phase, (dev - gid + DEVICES) % DEVICES],
-            recv_sem=sync_recv.at[phase, slot],
-            device_id=coords(dev),
-            device_id_type=MESH,
-        )
+    def tile_copies(phase):
+        return [
+            pltpu.make_async_remote_copy(
+                src_ref=sync_src.at[phase],
+                dst_ref=sync_buf.at[phase, s],
+                send_sem=sync_send.at[phase, s],
+                recv_sem=sync_recv.at[phase, s],
+                device_id=peer,
+                device_id_type=MESH,
+            )
+            for s, peer in peers
+        ]
 
     def share(phase, tile):
         sync_src[phase] = tile
-        sync_buf[phase, pl.ds(gid, 1)] = tile[None]
-
-        def send(off, carry):
-            tile_copy(phase, gid, (gid + off) % DEVICES).start()
-            return carry
-
-        lax.fori_loop(1, DEVICES, send, 0)
+        for copy in tile_copies(phase):
+            copy.start()
+        sync_buf[phase, 0] = tile
 
     def collect(phase):
-        def receive(off, carry):
-            dev = (gid + DEVICES - off) % DEVICES
-            tile_copy(phase, dev, dev).wait_recv()
-            return carry
-
-        lax.fori_loop(1, DEVICES, receive, 0)
+        for copy in tile_copies(phase):
+            copy.wait_recv()
         return jnp.sum(sync_buf[phase], axis=0)
 
     share(0, jnp.sum(n_acc[:, :LANES] + n_acc[:, LANES:], axis=0, keepdims=True))
@@ -340,18 +333,14 @@
     replica_copy(0).start()
     set_ratio(weight_sq, collect(3))
     ratio_copy.start()
+    lax.fori_loop(0, HEAD, send_late, 0)
     for i in range(1, len(CHUNKS)):
         lax.fori_loop(starts[i], starts[i] + CHUNKS[i], finish, 0)
         replica_copy(i).start()
-        if i == LATE:
-            lax.fori_loop(0, HEAD, send_late, 0)
-
-    def drain(off, carry):
-        for phase in range(PHASES):
-            tile_copy(phase, gid, (gid + off) % DEVICES).wait_send()
-        return carry
-
-    lax.fori_loop(1, DEVICES, drain, 0)
+
+    for phase in range(PHASES):
+        for copy in tile_copies(phase):
+            copy.wait_send()
     coef_copy.wait()
     ratio_copy.wait()
     for group in range(LAYERS // GROUP):

time: 274 us -> 274 us (level)
  no operation moved by 1% of the time
where the time goes in v4:
time: 274 us; the launch traced here: 273 us
  Pallas kernels  204 us (74%)
  waiting for transfers between devices  54.7 us (20%)
  local copies, waits for them, and re-layouts  7.13 us (3%)
  starting transfers between devices  6.17 us (2%)
    pallas_call x1, Pallas kernels, run_step(): pl.pallas_call(step_kernel, out_shape=out_shape, in_specs=[anywhere] * (K...  168 us
    ppermute x4, waiting for transfers between devices, device_step(): far = lax.ppermute(own, 'data', across) if chunk else far_head  48.7 us
    pallas_call x1, Pallas kernels, update(): pl.pallas_call(update_kernel, grid=(LAYERS // block,), out_shape=[jax.Sha...  22.2 us
    pallas_call x5, Pallas kernels, assemble(): pl.pallas_call(functools.partial(assemble_kernel, bool(previous)), grid=(...  13.8 us
    unnamed x24, local copies, waits for them, and re-layouts  7.13 us
    ppermute x5, waiting for transfers between devices, device_step(): far_near = lax.ppermute(far, 'data', on_chip)  5.96 us
  transfers between devices with their start and end apart: 14, of which 2 were waited for; matrix products, arithmetic and copies ran while one was open for 0% of the time, Pallas kernels for 12%

profile of v4, /device:TPU:0, one launch (start us, length us, event | category | flops | bytes accessed | tf_op | source)
XLA Modules:
  0.0 272.7 jit_solution(16303854950623184737)
XLA Ops:
  0.6 167.9 %lamb_step.1 = (f32[32,64,192]{2,1,0:T(8,128)}, f32[32,16,256]{2,1,0:T(8,128)}, f32[32,64,256]{2,1,0:T(8,128)}, f32[32,64,256]{2,1,0:T(8,128)}, f32[1,128]{1,0:T...) custom-call(f32[1,32,192,256]{3,2,1,0:T(8,128)} %bitcast.3, ...), custom_call_target="tpu_custom_call" | custom-call | tf_op jit(solution)/shard_map/lamb_step/pallas_call | solution.py:373
  168.5 1.3 collective-permute-start.9
  169.8 0.8 collective-permute-start.6
  170.6 1.3 collective-permute-start.3
  171.9 0.0 collective-permute-start.12
  171.9 0.8 collective-permute-start
  172.6 48.7 %collective-permute-done.refs_1_ = bf16[2,192,256]{2,1,0:T(8,128)(2,1)S(1)} collective-permute-done((bf16[2,192,256]{2,1,0:T(8,128)(2,1)}, bf16[2,192,256]{2,1,0:T(8,128)(2,1)S(1)}, u32[]{:S(2)}, u32[]{:S(2)}) %collective-permute-start) | collective-permute-done | bytes 196640 | tf_op jit(solution)/shard_map/ppermute | solution.py:474
  221.3 0.0 collective-permute-start.10
  221.3 0.0 collective-permute-done.3.refs_1_
  221.3 0.5 collective-permute-start.7
  221.9 0.0 collective-permute-done.9.refs_1_
  221.9 0.0 collective-permute-start.11
  221.9 0.0 collective-permute-done.6.refs_1_
  221.9 0.5 collective-permute-start.8
  222.4 0.0 collective-permute-done.12.refs_2_
  222.4 0.0 copy-start.6
  222.4 0.8 copy-done.6
  223.2 0.0 collective-permute-start.13
  223.2 5.9 %collective-permute-done.13.refs_3_ = bf16[6,192,256]{2,1,0:T(8,128)(2,1)S(1)} collective-permute-done((bf16[6,192,256]{2,1,0:T(8,128)(2,1)}, bf16[6,192,256]{2,1,0:T(8,128)(2,1)S(1)}, u32[]{:S(2)}, u32[]{:S(2)}) %collective-permute-start.13) | collective-permute-done | bytes 589856 | tf_op jit(solution)/shard_map/ppermute | solution.py:476
  229.2 0.0 copy-start.8
  229.2 0.8 copy-done.8
  230.0 0.1 collective-permute-start.4
  230.1 0.0 collective-permute-done.10.refs_2_
  230.1 0.4 collective-permute-start.5
  230.5 0.0 collective-permute-done.7.refs_2_
  230.5 0.1 collective-permute-start.1
  230.6 0.0 collective-permute-done.11.refs_3_
  230.7 0.0 copy-start.2
  230.7 1.0 copy-done.2
  231.6 0.4 collective-permute-start.2
  232.0 22.2 %update.1 = (f32[32,64,192]{2,1,0:T(8,128)}, f32[32,16,256]{2,1,0:T(8,128)}, f32[32,64,256]{2,1,0:T(8,128)}, f32[32,64,256]{2,1,0:T(8,128)}, f32[32,64,192]{2,1,...) custom-call(f32[1,128]{1,0:T(1,128)} %get-tuple-element.86.refs_0_, ...), custom_call_target="tpu_custom_call" | custom-call | flops 2000000000 | bytes 47000000 | tf_op jit(solution)/shard_map/update/pallas_call | solution.py:405
  254.2 0.0 copy-start.4
  254.2 1.1 copy-done.4
  255.3 0.0 copy-start.5
  255.3 1.1 copy-done.5
  256.4 0.0 copy-start.7
  256.4 1.1 copy-done.7
  257.4 0.0 copy-start.9
  257.4 1.1 copy-done.9
  258.5 0.0 copy-start.1
  258.5 0.0 copy-start.3
  258.5 1.9 assemble.5
  260.4 0.0 copy-done.1
  260.4 0.3 copy-done.3
  260.7 0.0 copy-start
  260.7 2.9 %assemble.6 = (bf16[32,192,256]{2,1,0:T(8,128)(2,1)}, bf16[32,64,256]{2,1,0:T(8,128)(2,1)}, bf16[32,256,256]{2,1,0:T(8,128)(2,1)}, bf16[32,256,256]{2,1,0:T(8,128)(2,1)}) custom-call(bf16[10,192,256]{2,1,0:T(8,128)(2,1)S(1)} %copy-done.1, ...), custom_call_target="tpu_custom_call", output_to_operand_aliasing={{0}: (4, {}), {1}: (5, {}), {2}: (6, {}), {3}: (7, {})} | custom-call | flops 400000000 | bytes 8000000 | tf_op jit(solution)/shard_map/assemble/pallas_call | solution.py:444
  263.6 0.0 collective-permute-done.8.refs_3_
  263.6 0.0 copy-done
  263.6 0.0 copy-start.10
  263.6 4.6 %assemble.7 = (bf16[32,192,256]{2,1,0:T(8,128)(2,1)}, bf16[32,64,256]{2,1,0:T(8,128)(2,1)}, bf16[32,256,256]{2,1,0:T(8,128)(2,1)}, bf16[32,256,256]{2,1,0:T(8,128)(2,1)}) custom-call(bf16[10,192,256]{2,1,0:T(8,128)(2,1)S(1)} %copy-done, ...), custom_call_target="tpu_custom_call", output_to_operand_aliasing={{0}: (4, {}), {1}: (5, {}), {2}: (6, {}), {3}: (7, {})} | custom-call | flops 400000000 | bytes 8000000 | tf_op jit(solution)/shard_map/assemble/pallas_call | solution.py:444
  268.2 0.0 collective-permute-done.4.refs_2_
  268.2 0.0 collective-permute-done.5.refs_3_
  268.2 0.0 copy-done.10
  268.3 0.0 copy-start.11
  268.3 2.4 assemble.8
  270.7 0.0 collective-permute-done.1.refs_2_
  270.7 0.0 collective-permute-done.2.refs_3_
  270.7 0.0 copy-done.11
  270.7 2.0 assemble.9
Async XLA Ops:
  168.5 53.3 %collective-permute-start.9 = (bf16[10,192,256]{2,1,0:T(8,128)(2,1)}, bf16[10,192,256]{2,1,0:T(8,128)(2,1)S(1)}, u32[]{:S(2)}, u32[]{:S(2)}) collective-permute-start(bf16[10,192,256]{2,1,0:T(8,128)(2,1)} %get-tuple-element.63.refs_0_), channel_id=1, source_target_pairs={{0,2},{1,3},{2,0},{3,1},{4,6},{5,7},{6,4},{7,5},{8,10},{9,11},{10,... | collective-permute-start | bytes 2949128 | tf_op jit(solution)/shard_map/ppermute | solution.py:474
  169.8 52.1 %collective-permute-start.6 = (bf16[10,192,256]{2,1,0:T(8,128)(2,1)}, bf16[10,192,256]{2,1,0:T(8,128)(2,1)S(1)}, u32[]{:S(2)}, u32[]{:S(2)}) collective-permute-start(bf16[10,192,256]{2,1,0:T(8,128)(2,1)} %get-tuple-element.62.refs_0_), channel_id=1, source_target_pairs={{0,2},{1,3},{2,0},{3,1},{4,6},{5,7},{6,4},{7,5},{8,10},{9,11},{10,... | collective-permute-start | bytes 2949128 | tf_op jit(solution)/shard_map/ppermute | solution.py:474
  170.6 50.7 %collective-permute-start.3 = (bf16[4,192,256]{2,1,0:T(8,128)(2,1)}, bf16[4,192,256]{2,1,0:T(8,128)(2,1)}, u32[]{:S(2)}, u32[]{:S(2)}) collective-permute-start(bf16[4,192,256]{2,1,0:T(8,128)(2,1)} %get-tuple-element.61.refs_0_), channel_id=1, source_target_pairs={{0,2},{1,3},{2,0},{3,1},{4,6},{5,7},{6,4},{7,5},{8,10},{9,11},{10,... | collective-permute-start | bytes 1179656 | tf_op jit(solution)/shard_map/ppermute | solution.py:474
  171.9 50.5 %collective-permute-start.12 = (bf16[6,192,256]{2,1,0:T(8,128)(2,1)}, bf16[6,192,256]{2,1,0:T(8,128)(2,1)S(1)}, u32[]{:S(2)}, u32[]{:S(2)}) collective-permute-start(bf16[6,192,256]{2,1,0:T(8,128)(2,1)} %get-tuple-element.64.refs_0_), channel_id=1, source_target_pairs={{0,1},{1,0},{2,3},{3,2},{4,5},{5,4},{6,7},{7,6},{8,9},{9,8},{10,11... | collective-permute-start | bytes 1769480 | tf_op jit(solution)/shard_map/ppermute | solution.py:475
  171.9 49.5 %collective-permute-start = (bf16[2,192,256]{2,1,0:T(8,128)(2,1)}, bf16[2,192,256]{2,1,0:T(8,128)(2,1)S(1)}, u32[]{:S(2)}, u32[]{:S(2)}) collective-permute-start(bf16[2,192,256]{2,1,0:T(8,128)(2,1)} %get-tuple-element.60.refs_0_), channel_id=1, source_target_pairs={{0,2},{1,3},{2,0},{3,1},{4,6},{5,7},{6,4},{7,5},{8,10},{9,11},{10,... | collective-permute-start | bytes 589832 | tf_op jit(solution)/shard_map/ppermute | solution.py:474
  221.3 8.8 %collective-permute-start.10 = (bf16[10,192,256]{2,1,0:T(8,128)(2,1)}, bf16[10,192,256]{2,1,0:T(8,128)(2,1)S(1)}, u32[]{:S(2)}, u32[]{:S(2)}) collective-permute-start(bf16[10,192,256]{2,1,0:T(8,128)(2,1)} %get-tuple-element.63.refs_0_), channel_id=1, source_target_pairs={{0,1},{1,0},{2,3},{3,2},{4,5},{5,4},{6,7},{7,6},{8,9},{9,8},{10,11... | collective-permute-start | bytes 2949128 | tf_op jit(solution)/shard_map/ppermute | solution.py:475
  221.3 9.2 %collective-permute-start.7 = (bf16[10,192,256]{2,1,0:T(8,128)(2,1)}, bf16[10,192,256]{2,1,0:T(8,128)(2,1)S(1)}, u32[]{:S(2)}, u32[]{:S(2)}) collective-permute-start(bf16[10,192,256]{2,1,0:T(8,128)(2,1)} %get-tuple-element.62.refs_0_), channel_id=1, source_target_pairs={{0,1},{1,0},{2,3},{3,2},{4,5},{5,4},{6,7},{7,6},{8,9},{9,8},{10,11... | collective-permute-start | bytes 2949128 | tf_op jit(solution)/shard_map/ppermute | solution.py:475
  221.9 8.8 %collective-permute-start.11 = (bf16[10,192,256]{2,1,0:T(8,128)(2,1)S(1)}, bf16[10,192,256]{2,1,0:T(8,128)(2,1)S(1)}, u32[]{:S(2)}, u32[]{:S(2)}) collective-permute-start(bf16[10,192,256]{2,1,0:T(8,128)(2,1)S(1)} %collective-permute-done.9.refs_1_), channel_id=1, source_target_pairs={{0,1},{1,0},{2,3},{3,2},{4,5},{5,4},{6,7},{7,6},{8,9},{9,8},{10,11... | collective-permute-start | bytes 2949128 | tf_op jit(solution)/shard_map/ppermute | solution.py:476
  221.9 41.7 %collective-permute-start.8 = (bf16[10,192,256]{2,1,0:T(8,128)(2,1)S(1)}, bf16[10,192,256]{2,1,0:T(8,128)(2,1)}, u32[]{:S(2)}, u32[]{:S(2)}) collective-permute-start(bf16[10,192,256]{2,1,0:T(8,128)(2,1)S(1)} %collective-permute-done.6.refs_1_), channel_id=1, source_target_pairs={{0,1},{1,0},{2,3},{3,2},{4,5},{5,4},{6,7},{7,6},{8,9},{9,8},{10,11... | collective-permute-start | bytes 2949128 | tf_op jit(solution)/shard_map/ppermute | solution.py:476
  222.4 0.8 copy-start.6
  223.2 6.0 %collective-permute-start.13 = (bf16[6,192,256]{2,1,0:T(8,128)(2,1)}, bf16[6,192,256]{2,1,0:T(8,128)(2,1)S(1)}, u32[]{:S(2)}, u32[]{:S(2)}) collective-permute-start(bf16[6,192,256]{2,1,0:T(8,128)(2,1)} %get-tuple-element.65.refs_1_), channel_id=1, source_target_pairs={{0,1},{1,0},{2,3},{3,2},{4,5},{5,4},{6,7},{7,6},{8,9},{9,8},{10,11... | collective-permute-start | bytes 1769480 | tf_op jit(solution)/shard_map/ppermute | solution.py:476
  229.2 0.8 copy-start.8
  230.0 38.2 %collective-permute-start.4 = (bf16[4,192,256]{2,1,0:T(8,128)(2,1)}, bf16[4,192,256]{2,1,0:T(8,128)(2,1)}, u32[]{:S(2)}, u32[]{:S(2)}) collective-permute-start(bf16[4,192,256]{2,1,0:T(8,128)(2,1)} %get-tuple-element.61.refs_0_), channel_id=1, source_target_pairs={{0,1},{1,0},{2,3},{3,2},{4,5},{5,4},{6,7},{7,6},{8,9},{9,8},{10,11... | collective-permute-start | bytes 1179656 | tf_op jit(solution)/shard_map/ppermute | solution.py:475
  230.1 38.1 %collective-permute-start.5 = (bf16[4,192,256]{2,1,0:T(8,128)(2,1)}, bf16[4,192,256]{2,1,0:T(8,128)(2,1)}, u32[]{:S(2)}, u32[]{:S(2)}) collective-permute-start(bf16[4,192,256]{2,1,0:T(8,128)(2,1)} %collective-permute-done.3.refs_1_), channel_id=1, source_target_pairs={{0,1},{1,0},{2,3},{3,2},{4,5},{5,4},{6,7},{7,6},{8,9},{9,8},{10,11... | collective-permute-start | bytes 1179656 | tf_op jit(solution)/shard_map/ppermute | solution.py:476
  230.5 40.1 %collective-permute-start.1 = (bf16[2,192,256]{2,1,0:T(8,128)(2,1)}, bf16[2,192,256]{2,1,0:T(8,128)(2,1)}, u32[]{:S(2)}, u32[]{:S(2)}) collective-permute-start(bf16[2,192,256]{2,1,0:T(8,128)(2,1)} %get-tuple-element.60.refs_0_), channel_id=1, source_target_pairs={{0,1},{1,0},{2,3},{3,2},{4,5},{5,4},{6,7},{7,6},{8,9},{9,8},{10,11... | collective-permute-start | bytes 589832 | tf_op jit(solution)/shard_map/ppermute | solution.py:475
  230.7 1.0 copy-start.2
  231.6 39.1 %collective-permute-start.2 = (bf16[2,192,256]{2,1,0:T(8,128)(2,1)S(1)}, bf16[2,192,256]{2,1,0:T(8,128)(2,1)}, u32[]{:S(2)}, u32[]{:S(2)}) collective-permute-start(bf16[2,192,256]{2,1,0:T(8,128)(2,1)S(1)} %collective-permute-done.refs_1_), channel_id=1, source_target_pairs={{0,1},{1,0},{2,3},{3,2},{4,5},{5,4},{6,7},{7,6},{8,9},{9,8},{10,11... | collective-permute-start | bytes 589832 | tf_op jit(solution)/shard_map/ppermute | solution.py:476
  254.2 1.1 copy-start.4
  255.3 1.1 copy-start.5
  256.4 1.1 copy-start.7
  257.4 1.1 copy-start.9
  258.5 1.9 copy-start.1
  258.5 2.2 copy-start.3
  260.7 2.9 %copy-start = (bf16[10,192,256]{2,1,0:T(8,128)(2,1)S(1)}, bf16[10,192,256]{2,1,0:T(8,128)(2,1)}, u32[]{:S(2)}) copy-start(bf16[10,192,256]{2,1,0:T(8,128)(2,1)} %get-tuple-element.62.refs_0_) | copy-start | bytes 2949124
  263.6 4.6 %copy-start.10 = (bf16[4,192,256]{2,1,0:T(8,128)(2,1)S(1)}, bf16[4,192,256]{2,1,0:T(8,128)(2,1)}, u32[]{:S(2)}) copy-start(bf16[4,192,256]{2,1,0:T(8,128)(2,1)} %get-tuple-element.61.refs_0_) | copy-start | bytes 1179652
  268.3 2.4 copy-start.11
